TPU v7x, 8 devices: a whole 2x2x1 slice. The times are simulated.
8 devices in a mesh: dp: 1 (over z), sp: 2 (over y), cp: 4 (over x, core).
Axes of the slice: x: 2, y: 2, z: 1, core: 2. Of those that a mesh axis runs over, the one named last changes fastest.
Arguments:
- x_chunk: bfloat16 [512, 16384], P(('dp', 'sp', 'cp'))
- k_cache: bfloat16 [32768, 8, 128], P(('dp', 'sp', 'cp'))
- v_cache: bfloat16 [32768, 8, 128], P(('dp', 'sp', 'cp'))
- w_q: bfloat16 [16384, 16384], replicated
- w_k: bfloat16 [16384, 1024], replicated
- w_v: bfloat16 [16384, 1024], replicated
- w_o: bfloat16 [16384, 16384], replicated
Outputs:
- output 1: bfloat16 [512, 16384], P(('dp', 'sp', 'cp'))
- output 2: bfloat16 [512, 8, 128], P(('dp', 'sp', 'cp'))
- output 3: bfloat16 [512, 8, 128], P(('dp', 'sp', 'cp'))
All inputs are finite; a program needn't handle non-finite values.
Results may differ from a plain program's by a relative error of at most 0.00585936.
Values are sent between devices in bfloat16 or wider.
A program may use at most 4.5 GiB of HBM per device.

v0:
```python
import jax
import jax.numpy as jnp
from jax import lax
from jax.sharding import PartitionSpec as P

ROPE_BASE = 500000
SEQ_AXES = ('sp', 'cp')


def rope_tables(positions, head_dim):
    inv_freq = 1.0 / (ROPE_BASE ** (jnp.arange(0, head_dim, 2, dtype=jnp.float32) / head_dim))
    angles = positions.astype(jnp.float32)[:, None] * inv_freq[None, :]
    return jnp.cos(angles), jnp.sin(angles)


def apply_rope(values, cos_t, sin_t):
    half_dim = values.shape[-1] // 2
    lo_half = values[..., :half_dim].astype(jnp.float32)
    hi_half = values[..., half_dim:].astype(jnp.float32)
    return jnp.concatenate([lo_half * cos_t - hi_half * sin_t, hi_half * cos_t + lo_half * sin_t], axis=-1).astype(jnp.bfloat16)


def attend_block(q_grp, keys, values, attn_scale, allowed=None):
    scores = jnp.einsum('qhgd,khd->hgqk', q_grp, keys, preferred_element_type=jnp.float32) * attn_scale
    if allowed is not None:
        scores = jnp.where(allowed, scores, -jnp.inf)
    row_max = jnp.max(scores, axis=-1)
    exp_scores = jnp.exp(scores - row_max[..., None])
    row_sum = jnp.sum(exp_scores, axis=-1)
    out_part = jnp.einsum('hgqk,khd->hgqd', exp_scores.astype(jnp.bfloat16), values, preferred_element_type=jnp.float32) / row_sum[..., None]
    return out_part, row_max + jnp.log(row_sum)


def merge_parts(out_a, lse_a, out_b, lse_b):
    lse_new = jnp.logaddexp(lse_a, lse_b)
    return out_a * jnp.exp(lse_a - lse_new)[..., None] + out_b * jnp.exp(lse_b - lse_new)[..., None], lse_new


def project_rows(x_loc, w_q, w_k, w_v, kv_heads, head_dim, positions):
    tok_loc = x_loc.shape[0]
    group_size = w_q.shape[1] // (kv_heads * head_dim)
    cos_t, sin_t = rope_tables(positions, head_dim)
    q_rows = jnp.dot(x_loc, w_q, preferred_element_type=jnp.float32).astype(jnp.bfloat16)
    q_grp = apply_rope(q_rows.reshape(tok_loc, kv_heads, group_size, head_dim), cos_t[:, None, None, :], sin_t[:, None, None, :])
    k_rows = jnp.dot(x_loc, w_k, preferred_element_type=jnp.float32).astype(jnp.bfloat16)
    k_new = apply_rope(k_rows.reshape(tok_loc, kv_heads, head_dim), cos_t[:, None, :], sin_t[:, None, :])
    v_new = jnp.dot(x_loc, w_v, preferred_element_type=jnp.float32).astype(jnp.bfloat16).reshape(tok_loc, kv_heads, head_dim)
    return q_grp, k_new, v_new


def solution(mesh):
    seq_size = mesh.shape['sp'] * mesh.shape['cp']
    cp_size = mesh.shape['cp']
    perm_next = [(src_idx, (src_idx + 1) % seq_size) for src_idx in range(seq_size)]
    row_spec = P(('dp', 'sp', 'cp'))

    def local_fn(x_loc, kc_loc, vc_loc, w_q, w_k, w_v, w_o):
        tok_loc, d_model = x_loc.shape
        cache_loc, kv_heads, head_dim = kc_loc.shape
        group_size = w_q.shape[1] // (kv_heads * head_dim)
        attn_scale = head_dim ** -0.5
        seq_idx = lax.axis_index('sp') * cp_size + lax.axis_index('cp')
        q_pos = seq_idx * tok_loc + jnp.arange(tok_loc)
        q_grp, k_new, v_new = project_rows(x_loc, w_q, w_k, w_v, kv_heads, head_dim, cache_loc * seq_size + q_pos)
        diag_mask = jnp.arange(tok_loc)[None, :] <= jnp.arange(tok_loc)[:, None]
        acc_out, acc_lse = attend_block(q_grp, k_new, v_new, attn_scale, diag_mask)
        k_fresh = lax.all_gather(k_new, SEQ_AXES, axis=0, tiled=True)
        v_fresh = lax.all_gather(v_new, SEQ_AXES, axis=0, tiled=True)

        def earlier_step(blk_idx, acc_state):
            k_blk = lax.dynamic_slice_in_dim(k_fresh, blk_idx * tok_loc, tok_loc, axis=0)
            v_blk = lax.dynamic_slice_in_dim(v_fresh, blk_idx * tok_loc, tok_loc, axis=0)
            out_part, lse_part = attend_block(q_grp, k_blk, v_blk, attn_scale)
            return merge_parts(acc_state[0], acc_state[1], out_part, lse_part)

        acc_out, acc_lse = lax.fori_loop(0, seq_idx, earlier_step, (acc_out, acc_lse))
        out_part, lse_part = attend_block(q_grp, kc_loc, vc_loc, attn_scale)
        acc_out, acc_lse = merge_parts(acc_out, acc_lse, out_part, lse_part)

        def cache_step(step_idx, loop_state):
            k_blk, v_blk, acc_o, acc_l = loop_state
            k_blk = lax.ppermute(k_blk, SEQ_AXES, perm_next)
            v_blk = lax.ppermute(v_blk, SEQ_AXES, perm_next)
            part_o, part_l = attend_block(q_grp, k_blk, v_blk, attn_scale)
            acc_o, acc_l = merge_parts(acc_o, acc_l, part_o, part_l)
            return k_blk, v_blk, acc_o, acc_l

        loop_state = lax.fori_loop(1, seq_size, cache_step, (kc_loc, vc_loc, acc_out, acc_lse))
        attn_bf = loop_state[2].astype(jnp.bfloat16)
        w_heads = w_o.reshape(kv_heads, group_size, head_dim, d_model)
        y_loc = jnp.einsum('hgqd,hgdm->qm', attn_bf, w_heads, preferred_element_type=jnp.float32).astype(jnp.bfloat16)
        return y_loc, k_new, v_new

    return jax.shard_map(local_fn, mesh=mesh, in_specs=(row_spec, row_spec, row_spec, P(), P(), P(), P()), out_specs=(row_spec, row_spec, row_spec), check_vma=False)
```

profile of v0, /device:TPU:0, one launch (start us, length us, event | category | flops | bytes accessed | tf_op | source)
XLA Modules:
  0.0 2367.7 jit_solution(7002950627276679262)
XLA Ops:
  8.8 13.6 fusion.66
  24.2 13.6 fusion.67
  38.5 165.0 %fusion.63 = bf16[8,8,128,128]{3,1,2,0:T(8,128)(2,1)} fusion(bf16[64,16384]{1,0:T(8,128)(2,1)S(1)} %copy-done, bf16[16384,16384]{1,0:T(8,128)(2,1)} %param.14), kind=kOutput, calls=%fused_computation.73 | convolution fusion | flops 34360786944 | bytes 541065216 | tf_op jit(solution)/shard_map/dot_general | solution.py:43
  206.7 7.7 copy.65
  218.4 48.8 %bitcast_reduce_fusion.2 = (f32[8,16,64]{1,2,0:T(8,128)S(1)}, f32[8,64,16,4096]{3,2,1,0:T(8,128)}) fusion(bf16[4096,8,128,1]{2,1,0,3:T(8,128)(2,1)} %bitcast.135, bf16[64,8,16,128]{3,0,2,1:T(8,128)(2,1)S(1)} %pad_maximum_fusion), kind=kOutput, calls=%fused_computation.38 | convolution fusion | flops 8657035264 | bytes 144736256 | tf_op jit(solution)/shard_map/qhgd,khd->hgqk/dot_general | solution.py:24
  267.3 41.3 %fusion.31 = f32[8,16,64]{1,2,0:T(8,128)S(1)} fusion(f32[8,64,16,4096]{3,2,1,0:T(8,128)} %get-tuple-element.174, f32[8,16,64]{1,2,0:T(8,128)S(1)} %get-tuple-element.173), kind=kLoop, calls=%fused_computation.41 | loop fusion | flops 100655104 | bytes 134283264 | tf_op jit(solution)/shard_map/reduce_sum | solution.py:29
  309.5 7.7 copy.66
  325.6 51.0 %fusion.47 = f32[8,16,64,128]{3,1,2,0:T(8,128)} fusion(f32[8,16,64,128]{3,2,1,0:T(8,128)} %get-tuple-element.74, bf16[4096,8,128,1]{2,1,0,3:T(8,128)(2,1)} %bitcast.137, f32[8,64,16,4096]{3,2,1,0:T(8,128)} %get-tuple-element.174, f32[8,16,64]{1,2,0:T(8,128)S(1)} %get-tuple-element.173, f32[8,16,64]{1,2,0:T(8,128)S(1)} %copy.64, ...), kind=kOutput, calls=%fused_computation.59 | convolution fusion | flops 8694792192 | bytes 151126016 | tf_op jit(solution)/shard_map/hgqk,khd->hgqd/dot_general | solution.py:30
  382.2 1813.8 %while.29 = (s32[]{:T(128)}, bf16[4096,8,128]{2,0,1:T(8,128)(2,1)}, bf16[4096,8,128]{2,0,1:T(8,128)(2,1)}, f32[8,16,64,128]{3,2,1,0:T(8,128)}, f32[8,16,64]{2,1,...) while((s32[]{:T(128)}, bf16[4096,8,128]{2,0,1:T(8,128)(2,1)}, ...), condition=%wide.region_11.12_spmd, body=%wide.region_8.11_spmd.sunk | while | flops 17452580864 | bytes 531103904 | solution.py:88
  382.4 14.9 collective-permute-start
  397.3 16.6 collective-permute-start.1
  414.0 161.7 %collective-permute-done = bf16[4096,8,128]{2,0,1:T(8,128)(2,1)} collective-permute-done((bf16[4096,8,128]{2,0,1:T(8,128)(2,1)}, bf16[4096,8,128]{2,0,1:T(8,128)(2,1)}, u32[]{:S(2)}, u32[]{:S(2)}) %collective-permute-start) | collective-permute-done | bytes 8388640 | tf_op jit(solution)/shard_map/while/body/eval_jaxpr/ppermute | solution.py:82
  575.6 47.0 %bitcast_reduce_fusion.6 = (f32[8,16,64]{2,1,0:T(8,128)S(1)}, f32[8,4096,64,16]{1,2,3,0:T(8,128)}) fusion(bf16[64,8,16,128]{3,0,2,1:T(8,128)(2,1)S(1)} %get-tuple-element.324, bf16[4096,8,128]{2,0,1:T(8,128)(2,1)} %collective-permute-done), kind=kOutput, calls=%fused_computation.21.clone.1 | convolution fusion | flops 8657035264 | bytes 144736256 | tf_op jit(solution)/shard_map/while/body/eval_jaxpr/qhgd,khd->hgqk/dot_general | solution.py:24
  622.6 7.2 copy.156
  629.9 41.1 %fusion.108 = f32[8,16,64]{2,1,0:T(8,128)S(1)} fusion(f32[8,4096,64,16]{1,2,3,0:T(8,128)} %get-tuple-element.268, f32[8,16,64]{2,1,0:T(8,128)S(1)} %get-tuple-element.269), kind=kLoop, calls=%fused_computation.24.clone.1 | loop fusion | flops 100655104 | bytes 134283264 | tf_op jit(solution)/shard_map/while/body/eval_jaxpr/reduce_sum | solution.py:29
  671.0 7.2 copy.157
  678.3 48.5 %multiply_add_fusion.5 = f32[8,16,64,128]{3,2,1,0:T(8,128)} fusion(f32[8,16,64,128]{3,2,1,0:T(8,128)} %get-tuple-element.315, bf16[4096,8,128]{2,0,1:T(8,128)(2,1)} %collective-permute-done.1, f32[8,4096,64,16]{1,2,3,0:T(8,128)} %get-tuple-element.268, f32[8,16,64]{2,1,0:T(8,128)S(1)} %get-tuple-element.269, ...), kind=kOutput, calls=%fused_computation.29.clone.1 | convolution fusion | flops 8694792192 | bytes 151126016 | tf_op jit(solution)/shard_map/while/body/eval_jaxpr/hgqk,khd->hgqd/dot_general | solution.py:30
  726.7 93.8 %collective-permute-done = bf16[4096,8,128]{2,0,1:T(8,128)(2,1)} collective-permute-done((bf16[4096,8,128]{2,0,1:T(8,128)(2,1)}, bf16[4096,8,128]{2,0,1:T(8,128)(2,1)}, u32[]{:S(2)}, u32[]{:S(2)}) %collective-permute-start) | collective-permute-done | bytes 8388640 | tf_op jit(solution)/shard_map/while/body/eval_jaxpr/ppermute | solution.py:82
  820.5 47.0 %bitcast_reduce_fusion.6 = (f32[8,16,64]{2,1,0:T(8,128)S(1)}, f32[8,4096,64,16]{1,2,3,0:T(8,128)}) fusion(bf16[64,8,16,128]{3,0,2,1:T(8,128)(2,1)S(1)} %get-tuple-element.324, bf16[4096,8,128]{2,0,1:T(8,128)(2,1)} %collective-permute-done), kind=kOutput, calls=%fused_computation.21.clone.1 | convolution fusion | flops 8657035264 | bytes 144736256 | tf_op jit(solution)/shard_map/while/body/eval_jaxpr/qhgd,khd->hgqk/dot_general | solution.py:24
  867.5 7.2 copy.156
  874.7 41.1 %fusion.108 = f32[8,16,64]{2,1,0:T(8,128)S(1)} fusion(f32[8,4096,64,16]{1,2,3,0:T(8,128)} %get-tuple-element.268, f32[8,16,64]{2,1,0:T(8,128)S(1)} %get-tuple-element.269), kind=kLoop, calls=%fused_computation.24.clone.1 | loop fusion | flops 100655104 | bytes 134283264 | tf_op jit(solution)/shard_map/while/body/eval_jaxpr/reduce_sum | solution.py:29
  923.1 48.5 %multiply_add_fusion.5 = f32[8,16,64,128]{3,2,1,0:T(8,128)} fusion(f32[8,16,64,128]{3,2,1,0:T(8,128)} %get-tuple-element.315, bf16[4096,8,128]{2,0,1:T(8,128)(2,1)} %collective-permute-done.1, f32[8,4096,64,16]{1,2,3,0:T(8,128)} %get-tuple-element.268, f32[8,16,64]{2,1,0:T(8,128)S(1)} %get-tuple-element.269, ...), kind=kOutput, calls=%fused_computation.29.clone.1 | convolution fusion | flops 8694792192 | bytes 151126016 | tf_op jit(solution)/shard_map/while/body/eval_jaxpr/hgqk,khd->hgqd/dot_general | solution.py:30
  971.6 93.8 %collective-permute-done = bf16[4096,8,128]{2,0,1:T(8,128)(2,1)} collective-permute-done((bf16[4096,8,128]{2,0,1:T(8,128)(2,1)}, bf16[4096,8,128]{2,0,1:T(8,128)(2,1)}, u32[]{:S(2)}, u32[]{:S(2)}) %collective-permute-start) | collective-permute-done | bytes 8388640 | tf_op jit(solution)/shard_map/while/body/eval_jaxpr/ppermute | solution.py:82
  1065.4 47.0 %bitcast_reduce_fusion.6 = (f32[8,16,64]{2,1,0:T(8,128)S(1)}, f32[8,4096,64,16]{1,2,3,0:T(8,128)}) fusion(bf16[64,8,16,128]{3,0,2,1:T(8,128)(2,1)S(1)} %get-tuple-element.324, bf16[4096,8,128]{2,0,1:T(8,128)(2,1)} %collective-permute-done), kind=kOutput, calls=%fused_computation.21.clone.1 | convolution fusion | flops 8657035264 | bytes 144736256 | tf_op jit(solution)/shard_map/while/body/eval_jaxpr/qhgd,khd->hgqk/dot_general | solution.py:24
  1112.4 7.2 copy.156
  1119.6 41.1 %fusion.108 = f32[8,16,64]{2,1,0:T(8,128)S(1)} fusion(f32[8,4096,64,16]{1,2,3,0:T(8,128)} %get-tuple-element.268, f32[8,16,64]{2,1,0:T(8,128)S(1)} %get-tuple-element.269), kind=kLoop, calls=%fused_computation.24.clone.1 | loop fusion | flops 100655104 | bytes 134283264 | tf_op jit(solution)/shard_map/while/body/eval_jaxpr/reduce_sum | solution.py:29
  1168.0 48.5 %multiply_add_fusion.5 = f32[8,16,64,128]{3,2,1,0:T(8,128)} fusion(f32[8,16,64,128]{3,2,1,0:T(8,128)} %get-tuple-element.315, bf16[4096,8,128]{2,0,1:T(8,128)(2,1)} %collective-permute-done.1, f32[8,4096,64,16]{1,2,3,0:T(8,128)} %get-tuple-element.268, f32[8,16,64]{2,1,0:T(8,128)S(1)} %get-tuple-element.269, ...), kind=kOutput, calls=%fused_computation.29.clone.1 | convolution fusion | flops 8694792192 | bytes 151126016 | tf_op jit(solution)/shard_map/while/body/eval_jaxpr/hgqk,khd->hgqd/dot_general | solution.py:30
  1216.5 93.8 %collective-permute-done = bf16[4096,8,128]{2,0,1:T(8,128)(2,1)} collective-permute-done((bf16[4096,8,128]{2,0,1:T(8,128)(2,1)}, bf16[4096,8,128]{2,0,1:T(8,128)(2,1)}, u32[]{:S(2)}, u32[]{:S(2)}) %collective-permute-start) | collective-permute-done | bytes 8388640 | tf_op jit(solution)/shard_map/while/body/eval_jaxpr/ppermute | solution.py:82
  1310.2 47.0 %bitcast_reduce_fusion.6 = (f32[8,16,64]{2,1,0:T(8,128)S(1)}, f32[8,4096,64,16]{1,2,3,0:T(8,128)}) fusion(bf16[64,8,16,128]{3,0,2,1:T(8,128)(2,1)S(1)} %get-tuple-element.324, bf16[4096,8,128]{2,0,1:T(8,128)(2,1)} %collective-permute-done), kind=kOutput, calls=%fused_computation.21.clone.1 | convolution fusion | flops 8657035264 | bytes 144736256 | tf_op jit(solution)/shard_map/while/body/eval_jaxpr/qhgd,khd->hgqk/dot_general | solution.py:24
  1357.3 7.2 copy.156
  1364.5 41.1 %fusion.108 = f32[8,16,64]{2,1,0:T(8,128)S(1)} fusion(f32[8,4096,64,16]{1,2,3,0:T(8,128)} %get-tuple-element.268, f32[8,16,64]{2,1,0:T(8,128)S(1)} %get-tuple-element.269), kind=kLoop, calls=%fused_computation.24.clone.1 | loop fusion | flops 100655104 | bytes 134283264 | tf_op jit(solution)/shard_map/while/body/eval_jaxpr/reduce_sum | solution.py:29
  1412.9 48.5 %multiply_add_fusion.5 = f32[8,16,64,128]{3,2,1,0:T(8,128)} fusion(f32[8,16,64,128]{3,2,1,0:T(8,128)} %get-tuple-element.315, bf16[4096,8,128]{2,0,1:T(8,128)(2,1)} %collective-permute-done.1, f32[8,4096,64,16]{1,2,3,0:T(8,128)} %get-tuple-element.268, f32[8,16,64]{2,1,0:T(8,128)S(1)} %get-tuple-element.269, ...), kind=kOutput, calls=%fused_computation.29.clone.1 | convolution fusion | flops 8694792192 | bytes 151126016 | tf_op jit(solution)/shard_map/while/body/eval_jaxpr/hgqk,khd->hgqd/dot_general | solution.py:30
  1461.3 93.8 %collective-permute-done = bf16[4096,8,128]{2,0,1:T(8,128)(2,1)} collective-permute-done((bf16[4096,8,128]{2,0,1:T(8,128)(2,1)}, bf16[4096,8,128]{2,0,1:T(8,128)(2,1)}, u32[]{:S(2)}, u32[]{:S(2)}) %collective-permute-start) | collective-permute-done | bytes 8388640 | tf_op jit(solution)/shard_map/while/body/eval_jaxpr/ppermute | solution.py:82
  1555.1 47.0 %bitcast_reduce_fusion.6 = (f32[8,16,64]{2,1,0:T(8,128)S(1)}, f32[8,4096,64,16]{1,2,3,0:T(8,128)}) fusion(bf16[64,8,16,128]{3,0,2,1:T(8,128)(2,1)S(1)} %get-tuple-element.324, bf16[4096,8,128]{2,0,1:T(8,128)(2,1)} %collective-permute-done), kind=kOutput, calls=%fused_computation.21.clone.1 | convolution fusion | flops 8657035264 | bytes 144736256 | tf_op jit(solution)/shard_map/while/body/eval_jaxpr/qhgd,khd->hgqk/dot_general | solution.py:24
  1602.1 7.2 copy.156
  1609.3 41.1 %fusion.108 = f32[8,16,64]{2,1,0:T(8,128)S(1)} fusion(f32[8,4096,64,16]{1,2,3,0:T(8,128)} %get-tuple-element.268, f32[8,16,64]{2,1,0:T(8,128)S(1)} %get-tuple-element.269), kind=kLoop, calls=%fused_computation.24.clone.1 | loop fusion | flops 100655104 | bytes 134283264 | tf_op jit(solution)/shard_map/while/body/eval_jaxpr/reduce_sum | solution.py:29
  1657.7 48.5 %multiply_add_fusion.5 = f32[8,16,64,128]{3,2,1,0:T(8,128)} fusion(f32[8,16,64,128]{3,2,1,0:T(8,128)} %get-tuple-element.315, bf16[4096,8,128]{2,0,1:T(8,128)(2,1)} %collective-permute-done.1, f32[8,4096,64,16]{1,2,3,0:T(8,128)} %get-tuple-element.268, f32[8,16,64]{2,1,0:T(8,128)S(1)} %get-tuple-element.269, ...), kind=kOutput, calls=%fused_computation.29.clone.1 | convolution fusion | flops 8694792192 | bytes 151126016 | tf_op jit(solution)/shard_map/while/body/eval_jaxpr/hgqk,khd->hgqd/dot_general | solution.py:30
  1706.2 93.8 %collective-permute-done = bf16[4096,8,128]{2,0,1:T(8,128)(2,1)} collective-permute-done((bf16[4096,8,128]{2,0,1:T(8,128)(2,1)}, bf16[4096,8,128]{2,0,1:T(8,128)(2,1)}, u32[]{:S(2)}, u32[]{:S(2)}) %collective-permute-start) | collective-permute-done | bytes 8388640 | tf_op jit(solution)/shard_map/while/body/eval_jaxpr/ppermute | solution.py:82
  1800.0 47.0 %bitcast_reduce_fusion.6 = (f32[8,16,64]{2,1,0:T(8,128)S(1)}, f32[8,4096,64,16]{1,2,3,0:T(8,128)}) fusion(bf16[64,8,16,128]{3,0,2,1:T(8,128)(2,1)S(1)} %get-tuple-element.324, bf16[4096,8,128]{2,0,1:T(8,128)(2,1)} %collective-permute-done), kind=kOutput, calls=%fused_computation.21.clone.1 | convolution fusion | flops 8657035264 | bytes 144736256 | tf_op jit(solution)/shard_map/while/body/eval_jaxpr/qhgd,khd->hgqk/dot_general | solution.py:24
  1847.0 7.2 copy.156
  1854.2 41.1 %fusion.108 = f32[8,16,64]{2,1,0:T(8,128)S(1)} fusion(f32[8,4096,64,16]{1,2,3,0:T(8,128)} %get-tuple-element.268, f32[8,16,64]{2,1,0:T(8,128)S(1)} %get-tuple-element.269), kind=kLoop, calls=%fused_computation.24.clone.1 | loop fusion | flops 100655104 | bytes 134283264 | tf_op jit(solution)/shard_map/while/body/eval_jaxpr/reduce_sum | solution.py:29
  1902.6 48.5 %multiply_add_fusion.5 = f32[8,16,64,128]{3,2,1,0:T(8,128)} fusion(f32[8,16,64,128]{3,2,1,0:T(8,128)} %get-tuple-element.315, bf16[4096,8,128]{2,0,1:T(8,128)(2,1)} %collective-permute-done.1, f32[8,4096,64,16]{1,2,3,0:T(8,128)} %get-tuple-element.268, f32[8,16,64]{2,1,0:T(8,128)S(1)} %get-tuple-element.269, ...), kind=kOutput, calls=%fused_computation.29.clone.1 | convolution fusion | flops 8694792192 | bytes 151126016 | tf_op jit(solution)/shard_map/while/body/eval_jaxpr/hgqk,khd->hgqd/dot_general | solution.py:30
  1951.1 93.8 %collective-permute-done = bf16[4096,8,128]{2,0,1:T(8,128)(2,1)} collective-permute-done((bf16[4096,8,128]{2,0,1:T(8,128)(2,1)}, bf16[4096,8,128]{2,0,1:T(8,128)(2,1)}, u32[]{:S(2)}, u32[]{:S(2)}) %collective-permute-start) | collective-permute-done | bytes 8388640 | tf_op jit(solution)/shard_map/while/body/eval_jaxpr/ppermute | solution.py:82
  2044.8 47.0 %bitcast_reduce_fusion.6 = (f32[8,16,64]{2,1,0:T(8,128)S(1)}, f32[8,4096,64,16]{1,2,3,0:T(8,128)}) fusion(bf16[64,8,16,128]{3,0,2,1:T(8,128)(2,1)S(1)} %get-tuple-element.324, bf16[4096,8,128]{2,0,1:T(8,128)(2,1)} %collective-permute-done), kind=kOutput, calls=%fused_computation.21.clone.1 | convolution fusion | flops 8657035264 | bytes 144736256 | tf_op jit(solution)/shard_map/while/body/eval_jaxpr/qhgd,khd->hgqk/dot_general | solution.py:24
  2091.9 7.2 copy.156
  2099.1 41.1 %fusion.108 = f32[8,16,64]{2,1,0:T(8,128)S(1)} fusion(f32[8,4096,64,16]{1,2,3,0:T(8,128)} %get-tuple-element.268, f32[8,16,64]{2,1,0:T(8,128)S(1)} %get-tuple-element.269), kind=kLoop, calls=%fused_computation.24.clone.1 | loop fusion | flops 100655104 | bytes 134283264 | tf_op jit(solution)/shard_map/while/body/eval_jaxpr/reduce_sum | solution.py:29
  2147.5 48.5 %multiply_add_fusion.5 = f32[8,16,64,128]{3,2,1,0:T(8,128)} fusion(f32[8,16,64,128]{3,2,1,0:T(8,128)} %get-tuple-element.315, bf16[4096,8,128]{2,0,1:T(8,128)(2,1)} %collective-permute-done.1, f32[8,4096,64,16]{1,2,3,0:T(8,128)} %get-tuple-element.268, f32[8,16,64]{2,1,0:T(8,128)S(1)} %get-tuple-element.269, ...), kind=kOutput, calls=%fused_computation.29.clone.1 | convolution fusion | flops 8694792192 | bytes 151126016 | tf_op jit(solution)/shard_map/while/body/eval_jaxpr/hgqk,khd->hgqd/dot_general | solution.py:30
  2196.0 164.5 %fusion.37 = bf16[64,16384]{1,0:T(8,128)(2,1)} fusion(bf16[8,16,128,16384]{3,2,1,0:T(8,128)(2,1)} %bitcast.17, f32[8,16,64,128]{3,2,1,0:T(8,128)} %get-tuple-element.76), kind=kOutput, calls=%fused_computation.44 | convolution fusion | flops 34361835520 | bytes 543162368 | tf_op jit(solution)/shard_map/hgqd,hgdm->qm/dot_general | solution.py:91
  (91 shorter events, 70.1 us)
Async XLA Ops:
  7.2 1.6 copy-start
  7.2 317.4 %all-gather.3.cloned.1.call-start = ((), (), s32[]{:S(2)}) async-start(), calls=%async_computation | async-start | bytes 1179648 | tf_op jit(solution)/shard_map/all_gather | solution.py:67
  22.7 0.6 copy-start.6
  22.7 0.6 copy-start.8
  24.1 300.5 %all-gather.5.cloned.1.call-start = ((), (), s32[]{:S(2)}) async-start(), calls=%async_computation.1 | async-start | bytes 1179648 | tf_op jit(solution)/shard_map/all_gather | solution.py:68
  206.6 7.7 copy-start.7
  206.7 7.7 copy-start.9
  267.3 41.3 %copy-start.4 = (bf16[64,8,128]{2,0,1:T(8,128)(2,1)S(1)}, bf16[64,8,128]{2,0,1:T(8,128)(2,1)}, u32[]{:S(2)}) copy-start(bf16[64,8,128]{2,0,1:T(8,128)(2,1)} %pad_maximum_fusion.1) | copy-start | bytes 393220
  317.2 3.6 copy-start.5
  324.7 0.6 copy-start.2
  376.6 5.5 copy-start.3
  382.4 193.2 %collective-permute-start = (bf16[4096,8,128]{2,0,1:T(8,128)(2,1)}, bf16[4096,8,128]{2,0,1:T(8,128)(2,1)}, u32[]{:S(2)}, u32[]{:S(2)}) collective-permute-start(bf16[4096,8,128]{2,0,1:T(8,128)(2,1)} %get-tuple-element.313), channel_id=1, source_target_pairs={{0,1},{1,2},{2,3},{3,4},{4,5},{5,6},{6,7},{7,0}} | collective-permute-start | bytes 25165832 | tf_op jit(solution)/shard_map/while/body/eval_jaxpr/ppermute | solution.py:82
  397.3 273.7 %collective-permute-start.1 = (bf16[4096,8,128]{2,0,1:T(8,128)(2,1)}, bf16[4096,8,128]{2,0,1:T(8,128)(2,1)}, u32[]{:S(2)}, u32[]{:S(2)}) collective-permute-start(bf16[4096,8,128]{2,0,1:T(8,128)(2,1)} %get-tuple-element.314), channel_id=1, source_target_pairs={{0,1},{1,2},{2,3},{3,4},{4,5},{5,6},{6,7},{7,0}} | collective-permute-start | bytes 25165832 | tf_op jit(solution)/shard_map/while/body/eval_jaxpr/ppermute | solution.py:83
  726.7 93.8 %collective-permute-start = (bf16[4096,8,128]{2,0,1:T(8,128)(2,1)}, bf16[4096,8,128]{2,0,1:T(8,128)(2,1)}, u32[]{:S(2)}, u32[]{:S(2)}) collective-permute-start(bf16[4096,8,128]{2,0,1:T(8,128)(2,1)} %get-tuple-element.313), channel_id=1, source_target_pairs={{0,1},{1,2},{2,3},{3,4},{4,5},{5,6},{6,7},{7,0}} | collective-permute-start | bytes 25165832 | tf_op jit(solution)/shard_map/while/body/eval_jaxpr/ppermute | solution.py:82
  726.7 189.2 %collective-permute-start.1 = (bf16[4096,8,128]{2,0,1:T(8,128)(2,1)}, bf16[4096,8,128]{2,0,1:T(8,128)(2,1)}, u32[]{:S(2)}, u32[]{:S(2)}) collective-permute-start(bf16[4096,8,128]{2,0,1:T(8,128)(2,1)} %get-tuple-element.314), channel_id=1, source_target_pairs={{0,1},{1,2},{2,3},{3,4},{4,5},{5,6},{6,7},{7,0}} | collective-permute-start | bytes 25165832 | tf_op jit(solution)/shard_map/while/body/eval_jaxpr/ppermute | solution.py:83
  971.6 93.8 %collective-permute-start = (bf16[4096,8,128]{2,0,1:T(8,128)(2,1)}, bf16[4096,8,128]{2,0,1:T(8,128)(2,1)}, u32[]{:S(2)}, u32[]{:S(2)}) collective-permute-start(bf16[4096,8,128]{2,0,1:T(8,128)(2,1)} %get-tuple-element.313), channel_id=1, source_target_pairs={{0,1},{1,2},{2,3},{3,4},{4,5},{5,6},{6,7},{7,0}} | collective-permute-start | bytes 25165832 | tf_op jit(solution)/shard_map/while/body/eval_jaxpr/ppermute | solution.py:82
  971.6 189.2 %collective-permute-start.1 = (bf16[4096,8,128]{2,0,1:T(8,128)(2,1)}, bf16[4096,8,128]{2,0,1:T(8,128)(2,1)}, u32[]{:S(2)}, u32[]{:S(2)}) collective-permute-start(bf16[4096,8,128]{2,0,1:T(8,128)(2,1)} %get-tuple-element.314), channel_id=1, source_target_pairs={{0,1},{1,2},{2,3},{3,4},{4,5},{5,6},{6,7},{7,0}} | collective-permute-start | bytes 25165832 | tf_op jit(solution)/shard_map/while/body/eval_jaxpr/ppermute | solution.py:83
  1216.5 93.8 %collective-permute-start = (bf16[4096,8,128]{2,0,1:T(8,128)(2,1)}, bf16[4096,8,128]{2,0,1:T(8,128)(2,1)}, u32[]{:S(2)}, u32[]{:S(2)}) collective-permute-start(bf16[4096,8,128]{2,0,1:T(8,128)(2,1)} %get-tuple-element.313), channel_id=1, source_target_pairs={{0,1},{1,2},{2,3},{3,4},{4,5},{5,6},{6,7},{7,0}} | collective-permute-start | bytes 25165832 | tf_op jit(solution)/shard_map/while/body/eval_jaxpr/ppermute | solution.py:82
  1216.5 189.2 %collective-permute-start.1 = (bf16[4096,8,128]{2,0,1:T(8,128)(2,1)}, bf16[4096,8,128]{2,0,1:T(8,128)(2,1)}, u32[]{:S(2)}, u32[]{:S(2)}) collective-permute-start(bf16[4096,8,128]{2,0,1:T(8,128)(2,1)} %get-tuple-element.314), channel_id=1, source_target_pairs={{0,1},{1,2},{2,3},{3,4},{4,5},{5,6},{6,7},{7,0}} | collective-permute-start | bytes 25165832 | tf_op jit(solution)/shard_map/while/body/eval_jaxpr/ppermute | solution.py:83
  1461.3 93.8 %collective-permute-start = (bf16[4096,8,128]{2,0,1:T(8,128)(2,1)}, bf16[4096,8,128]{2,0,1:T(8,128)(2,1)}, u32[]{:S(2)}, u32[]{:S(2)}) collective-permute-start(bf16[4096,8,128]{2,0,1:T(8,128)(2,1)} %get-tuple-element.313), channel_id=1, source_target_pairs={{0,1},{1,2},{2,3},{3,4},{4,5},{5,6},{6,7},{7,0}} | collective-permute-start | bytes 25165832 | tf_op jit(solution)/shard_map/while/body/eval_jaxpr/ppermute | solution.py:82
  1461.3 189.2 %collective-permute-start.1 = (bf16[4096,8,128]{2,0,1:T(8,128)(2,1)}, bf16[4096,8,128]{2,0,1:T(8,128)(2,1)}, u32[]{:S(2)}, u32[]{:S(2)}) collective-permute-start(bf16[4096,8,128]{2,0,1:T(8,128)(2,1)} %get-tuple-element.314), channel_id=1, source_target_pairs={{0,1},{1,2},{2,3},{3,4},{4,5},{5,6},{6,7},{7,0}} | collective-permute-start | bytes 25165832 | tf_op jit(solution)/shard_map/while/body/eval_jaxpr/ppermute | solution.py:83
  1706.2 93.8 %collective-permute-start = (bf16[4096,8,128]{2,0,1:T(8,128)(2,1)}, bf16[4096,8,128]{2,0,1:T(8,128)(2,1)}, u32[]{:S(2)}, u32[]{:S(2)}) collective-permute-start(bf16[4096,8,128]{2,0,1:T(8,128)(2,1)} %get-tuple-element.313), channel_id=1, source_target_pairs={{0,1},{1,2},{2,3},{3,4},{4,5},{5,6},{6,7},{7,0}} | collective-permute-start | bytes 25165832 | tf_op jit(solution)/shard_map/while/body/eval_jaxpr/ppermute | solution.py:82
  1706.2 189.2 %collective-permute-start.1 = (bf16[4096,8,128]{2,0,1:T(8,128)(2,1)}, bf16[4096,8,128]{2,0,1:T(8,128)(2,1)}, u32[]{:S(2)}, u32[]{:S(2)}) collective-permute-start(bf16[4096,8,128]{2,0,1:T(8,128)(2,1)} %get-tuple-element.314), channel_id=1, source_target_pairs={{0,1},{1,2},{2,3},{3,4},{4,5},{5,6},{6,7},{7,0}} | collective-permute-start | bytes 25165832 | tf_op jit(solution)/shard_map/while/body/eval_jaxpr/ppermute | solution.py:83
  1951.1 93.8 %collective-permute-start = (bf16[4096,8,128]{2,0,1:T(8,128)(2,1)}, bf16[4096,8,128]{2,0,1:T(8,128)(2,1)}, u32[]{:S(2)}, u32[]{:S(2)}) collective-permute-start(bf16[4096,8,128]{2,0,1:T(8,128)(2,1)} %get-tuple-element.313), channel_id=1, source_target_pairs={{0,1},{1,2},{2,3},{3,4},{4,5},{5,6},{6,7},{7,0}} | collective-permute-start | bytes 25165832 | tf_op jit(solution)/shard_map/while/body/eval_jaxpr/ppermute | solution.py:82
  1951.1 189.2 %collective-permute-start.1 = (bf16[4096,8,128]{2,0,1:T(8,128)(2,1)}, bf16[4096,8,128]{2,0,1:T(8,128)(2,1)}, u32[]{:S(2)}, u32[]{:S(2)}) collective-permute-start(bf16[4096,8,128]{2,0,1:T(8,128)(2,1)} %get-tuple-element.314), channel_id=1, source_target_pairs={{0,1},{1,2},{2,3},{3,4},{4,5},{5,6},{6,7},{7,0}} | collective-permute-start | bytes 25165832 | tf_op jit(solution)/shard_map/while/body/eval_jaxpr/ppermute | solution.py:83
  2195.9 164.5 %copy-start.1 = (bf16[64,16384]{1,0:T(8,128)(2,1)S(1)}, bf16[64,16384]{1,0:T(8,128)(2,1)}, u32[]{:S(2)}) copy-start(bf16[64,16384]{1,0:T(8,128)(2,1)} %param.11) | copy-start | bytes 6291460
Sparse Core Ops, SparseCore 0:
  24.2 20.3 all-gather.2
  47.1 17.5 all-gather.4
where the time goes:
time: 2380 us; the launch traced here: 2370 us
  matrix products  1130 us (47%)
  waiting for transfers between devices  724 us (30%)
  other arithmetic  336 us (14%)
  local copies, waits for them, and re-layouts  130 us (5%)
  starting transfers between devices  31.7 us (1%)
    ppermute x7, waiting for transfers between devices, cache_step(): k_blk = lax.ppermute(k_blk, SEQ_AXES, perm_next)  724 us
    dot_general x9, matrix products, attend_block(): jnp.einsum('hgqk,khd->hgqd', exp_scores.astype(jnp.bfloat16), values, pre...  394 us
    dot_general x9, matrix products, attend_block(): jnp.einsum('qhgd,khd->hgqk', q_grp, keys, preferred_element_type=jnp.floa...  380 us
    reduce_sum x9, other arithmetic, attend_block(): row_sum = jnp.sum(exp_scores, axis=-1)  330 us
    dot_general x1, matrix products, project_rows(): jnp.dot(x_loc, w_q, preferred_element_type=jnp.float32).astype(jnp.bfloat16)  165 us
    dot_general x1, matrix products, local_fn(): jnp.einsum('hgqd,hgdm->qm', attn_bf, w_heads, preferred_element_type=jnp....  164 us
    while x14, local copies, waits for them, and re-layouts  101 us
  transfers between devices with their start and end apart: 16, of which 7 were waited for; matrix products, arithmetic and copies ran while one was open for 41% of the time, Pallas kernels for 0%

commit v1 on v0

v1 whole, which is shorter than its diff:
```python
import functools
import jax
import jax.numpy as jnp
from jax import lax
from jax.experimental import pallas as pl
from jax.experimental.pallas import tpu as pltpu
from jax.sharding import PartitionSpec as P

ROPE_BASE = 500000
HD = 128
LOG2E = 1.4426950408889634
FLIPS = ((0, 0, 0), (0, 0, 1), (0, 1, 0), (1, 0, 0), (0, 1, 1), (1, 0, 1), (1, 1, 0), (1, 1, 1))


def rope_tables(positions):
    inv_freq = 1.0 / (ROPE_BASE ** (jnp.arange(0, HD, 2, dtype=jnp.float32) / HD))
    angles = positions.astype(jnp.float32)[:, None] * inv_freq[None, :]
    cos_t, sin_t = jnp.cos(angles), jnp.sin(angles)
    return jnp.concatenate([cos_t, cos_t], 1), jnp.concatenate([-sin_t, sin_t], 1)


def mm_kernel(off_ref, x_ref, w_ref, cos_ref, sin_ref, o_ref, *, rope, trans):
    acc = jnp.dot(x_ref[...], w_ref[...], preferred_element_type=jnp.float32).astype(jnp.bfloat16)
    if not rope:
        o_ref[...] = acc
        return
    for h in range(acc.shape[1] // HD):
        part = acc[:, h * HD:(h + 1) * HD].astype(jnp.float32)
        part = part * cos_ref[...] + pltpu.roll(part, HD // 2, 1) * sin_ref[...]
        if trans:
            o_ref[h * HD:(h + 1) * HD, :] = part.T.astype(jnp.bfloat16)
        else:
            o_ref[:, h * HD:(h + 1) * HD] = part.astype(jnp.bfloat16)


def matmul(x, w, cos_t, sin_t, off, n_cols, *, rope, trans=False, bn=256):
    rows, depth = x.shape
    out = (n_cols, rows) if trans else (rows, n_cols)
    ospec = pl.BlockSpec((bn, rows), lambda n, o: (n, 0)) if trans else pl.BlockSpec((rows, bn), lambda n, o: (0, n))
    return pl.pallas_call(
        functools.partial(mm_kernel, rope=rope, trans=trans),
        grid_spec=pltpu.PrefetchScalarGridSpec(
            num_scalar_prefetch=1,
            grid=(n_cols // bn,),
            in_specs=[
                pl.BlockSpec((rows, depth), lambda n, o: (0, 0), pipeline_mode=pl.Buffered(1)),
                pl.BlockSpec((depth, bn), lambda n, o: (0, o[0] + n)),
                pl.BlockSpec((rows, HD), lambda n, o: (0, 0)),
                pl.BlockSpec((rows, HD), lambda n, o: (0, 0)),
            ],
            out_specs=ospec,
        ),
        out_shape=jax.ShapeDtypeStruct(out, jnp.bfloat16),
        compiler_params=pltpu.CompilerParams(vmem_limit_bytes=48 << 20),
        cost_estimate=pl.CostEstimate(flops=2 * rows * depth * n_cols, bytes_accessed=2 * depth * n_cols, transcendentals=0),
    )(off, x, w, cos_t, sin_t)


def attn_kernel(kh_ref, vh_ref, qt_ref, kn_ref, vn_ref, o_ref,
                kb, vb, sbuf, acc, mst, lst, ksend, krecv, vsend, vrecv, *, tok, group, kblk, scale):
    cache = kb.shape[1]
    nsub = cache // kblk
    sp, cp = lax.axis_index('sp'), lax.axis_index('cp')
    chip, core = cp // 2, cp % 2
    cexp = scale * LOG2E

    def flip(v, f):
        return 1 - v if f else v

    def partner(p):
        fs, fx, fc = FLIPS[p]
        return flip(sp, fs), flip(chip, fx) * 2 + flip(core, fc)

    def dev(p):
        s, c = partner(p)
        return {'sp': s, 'cp': c}

    barrier = pltpu.get_barrier_semaphore()
    for p in range(1, 8):
        pl.semaphore_signal(barrier, inc=1, device_id=dev(p), device_id_type=pl.DeviceIdType.MESH)
    own = 2 * cp + sp
    k0 = pltpu.make_async_copy(kh_ref.at[own], kb.at[0], krecv.at[0])
    v0 = pltpu.make_async_copy(vh_ref.at[own], vb.at[0], vrecv.at[0])
    k0.start()
    v0.start()
    pl.semaphore_wait(barrier, 7)

    def remote(p):
        s, c = partner(p)
        head = 2 * c + s
        ck = pltpu.make_async_remote_copy(kh_ref.at[head], kb.at[p], ksend.at[p], krecv.at[p],
                                          device_id=dev(p), device_id_type=pl.DeviceIdType.MESH)
        cv = pltpu.make_async_remote_copy(vh_ref.at[head], vb.at[p], vsend.at[p], vrecv.at[p],
                                          device_id=dev(p), device_id_type=pl.DeviceIdType.MESH)
        return ck, cv

    for p in range(1, 8):
        ck, cv = remote(p)
        ck.start()
        cv.start()

    def q_of(h):
        return qt_ref[pl.ds(pl.multiple_of(h * HD, HD), HD), :]

    kpos = lax.broadcasted_iota(jnp.int32, (tok, tok), 0)
    qpos = lax.broadcasted_iota(jnp.int32, (tok, tok), 1)

    def first(h, carry):
        s = jnp.dot(kn_ref[...], q_of(h), preferred_element_type=jnp.float32)
        s = jnp.where(kpos <= qpos, s, -jnp.inf)
        m = jnp.max(s, axis=0, keepdims=True)
        p = jnp.exp2((s - m) * cexp)
        lst[h] = jnp.sum(p.reshape(tok // 8, 8, tok), axis=0)
        mst[h] = jnp.broadcast_to(m, (8, tok))
        acc[h] = jnp.dot(vn_ref[...], p.astype(jnp.bfloat16), preferred_element_type=jnp.float32)
        return carry

    lax.fori_loop(0, group, first, 0)

    def scores(slot, j, h, dst):
        keys = kb[slot, pl.ds(j * kblk, kblk), :]
        sbuf[dst] = jnp.dot(keys, q_of(h), preferred_element_type=jnp.float32)

    k0.wait()
    v0.wait()
    scores(0, 0, 0, 0)

    def step(i, carry):
        slot, h = i // group, i % group
        nxt = jnp.minimum(i + 1, 8 * group - 1)
        nslot, nh = nxt // group, nxt % group

        @pl.when((h == group - 1) & (slot < 7))
        def _():
            pltpu.make_async_copy(kb.at[nslot], kb.at[nslot], krecv.at[nslot]).wait()
            pltpu.make_async_copy(vb.at[nslot], vb.at[nslot], vrecv.at[nslot]).wait()

        m_run = mst[h, 0:1, :]
        l_run = lst[h]
        o_run = acc[h]
        for j in range(nsub):
            if j + 1 < nsub:
                scores(slot, j + 1, h, (j + 1) % 2)
            else:
                scores(nslot, 0, nh, (j + 1) % 2)
            s = sbuf[j % 2]
            m_new = jnp.maximum(m_run, jnp.max(s, axis=0, keepdims=True))
            alpha = jnp.exp2((m_run - m_new) * cexp)
            p = jnp.exp2((s - m_new) * cexp)
            l_run = l_run * alpha + jnp.sum(p.reshape(kblk // 8, 8, tok), axis=0)
            o_run = o_run * alpha + jnp.dot(vb[slot, :, pl.ds(j * kblk, kblk)], p.astype(jnp.bfloat16),
                                            preferred_element_type=jnp.float32)
            m_run = m_new
        mst[h] = jnp.broadcast_to(m_run, (8, tok))
        lst[h] = l_run
        acc[h] = o_run
        return carry

    lax.fori_loop(0, 8 * group, step, 0)

    def last(h, carry):
        total = jnp.sum(lst[h], axis=0, keepdims=True)
        o = acc[h] / total
        o_ref[:, pl.ds(pl.multiple_of(h * HD, HD), HD)] = o.T.astype(jnp.bfloat16)
        return carry

    lax.fori_loop(0, group, last, 0)
    for p in range(1, 8):
        ck, cv = remote(p)
        ck.wait_send()
        cv.wait_send()


def attention(kh, vh, qt, kn, vnt, kblk=512):
    n_kv, cache, _ = kh.shape
    group, tok = qt.shape[0] // HD, qt.shape[1]
    return pl.pallas_call(
        functools.partial(attn_kernel, tok=tok, group=group, kblk=kblk, scale=HD ** -0.5),
        in_specs=[pl.BlockSpec(memory_space=pl.ANY), pl.BlockSpec(memory_space=pl.ANY)] + [pl.BlockSpec(memory_space=pltpu.VMEM)] * 3,
        out_specs=pl.BlockSpec(memory_space=pltpu.VMEM),
        out_shape=jax.ShapeDtypeStruct((tok, group * HD), jnp.bfloat16),
        scratch_shapes=[
            pltpu.VMEM((8, cache, HD), jnp.bfloat16),
            pltpu.VMEM((8, HD, cache), jnp.bfloat16),
            pltpu.VMEM((2, kblk, tok), jnp.float32),
            pltpu.VMEM((group, HD, tok), jnp.float32),
            pltpu.VMEM((group, 8, tok), jnp.float32),
            pltpu.VMEM((group, 8, tok), jnp.float32),
            pltpu.SemaphoreType.DMA((8,)),
            pltpu.SemaphoreType.DMA((8,)),
            pltpu.SemaphoreType.DMA((8,)),
            pltpu.SemaphoreType.DMA((8,)),
        ],
        compiler_params=pltpu.CompilerParams(collective_id=0, has_side_effects=True, vmem_limit_bytes=60 << 20),
    )(kh, vh, qt, kn, vnt)


def solution(mesh):
    cp_size = mesh.shape['cp']
    row_spec = P(('dp', 'sp', 'cp'))

    def local_fn(x_loc, kc_loc, vc_loc, w_q, w_k, w_v, w_o):
        cache_loc, n_kv, _ = kc_loc.shape
        seq_size = mesh.shape['sp'] * cp_size
        sp, cp = lax.axis_index('sp'), lax.axis_index('cp')
        rows = x_loc.shape[0] * cp_size
        x_g = lax.all_gather(x_loc, 'cp', axis=0, tiled=True)
        cos_t, sin_t = rope_tables(cache_loc * seq_size + sp * rows + jnp.arange(rows))
        kh = jnp.transpose(kc_loc, (1, 0, 2))
        vh = jnp.transpose(vc_loc, (1, 2, 0))
        q_cols = w_q.shape[1] // cp_size
        k_cols = w_k.shape[1] // cp_size
        qoff = jnp.reshape(cp * (q_cols // 256), (1,)).astype(jnp.int32)
        koff = jnp.reshape(cp * (k_cols // 256), (1,)).astype(jnp.int32)
        k_part = matmul(x_g, w_k, cos_t, sin_t, koff, k_cols, rope=True)
        v_part = matmul(x_g, w_v, cos_t, sin_t, koff, k_cols, rope=False)
        qt = matmul(x_g, w_q, cos_t, sin_t, qoff, q_cols, rope=True, trans=True)
        kv = jnp.stack([k_part, v_part], 0)
        kv_rows = lax.all_to_all(kv, 'cp', split_axis=1, concat_axis=2, tiled=True)
        k_new = kv_rows[0].reshape(x_loc.shape[0], n_kv, HD)
        v_new = kv_rows[1].reshape(x_loc.shape[0], n_kv, HD)
        kv_head = lax.all_to_all(kv, 'sp', split_axis=2, concat_axis=1, tiled=True)
        qt = lax.all_to_all(qt, 'sp', split_axis=0, concat_axis=1, tiled=True)
        o = attention(kh, vh, qt, kv_head[0], kv_head[1].T)
        o = lax.all_to_all(o, 'sp', split_axis=0, concat_axis=1, tiled=True)
        o_g = lax.all_gather(o, 'cp', axis=1, tiled=True)
        y = matmul(o_g, w_o, cos_t, sin_t, qoff, q_cols, rope=False)
        y_loc = lax.all_to_all(y, 'cp', split_axis=0, concat_axis=1, tiled=True)
        return y_loc, k_new, v_new

    return jax.shard_map(local_fn, mesh=mesh, in_specs=(row_spec, row_spec, row_spec, P(), P(), P(), P()), out_specs=(row_spec, row_spec, row_spec), check_vma=False)
```

time: 2380 us -> 672 us (0.28)
  matrix products: 1130 us -> 0 us
  waiting for transfers between devices: 724 us -> 137 us
  Pallas kernels: 0 us -> 441 us
  other arithmetic: 336 us -> 0.72 us
  local copies, waits for them, and re-layouts: 130 us -> 31.9 us
  blocking collectives: 0 us -> 29.1 us
    dot_general x22 -> x0, matrix products: 1130 us -> none  [the longest x9 394 us: attend_block(): jnp.einsum('hgqk,khd->hgqd', exp_scores.astype(jnp.bfloat16), values, pre...]
    ppermute x14 -> x0, waiting for transfers between devices: 724 us -> none  [the longest x7 724 us: cache_step(): k_blk = lax.ppermute(k_blk, SEQ_AXES, perm_next)]
    pallas_call x0 -> x5, Pallas kernels: none -> 441 us  [the longest x1 317 us: attention(): pl.pallas_call(functools.partial(attn_kernel, tok=tok, group=group, kblk=...]
    reduce_sum x9 -> x0, other arithmetic: 330 us -> none  [attend_block(): row_sum = jnp.sum(exp_scores, axis=-1)]
    while x17 -> x0, local copies, waits for them, and re-layouts: 122 us -> none
    all_gather x2, waiting for transfers between devices: 0.01 us -> 112 us  [the longest x1 59.5 us: local_fn(): x_g = lax.all_gather(x_loc, 'cp', axis=0, tiled=True)]
    ppermute x14 -> x0, starting transfers between devices: 31.6 us -> none  [the longest x7 16.7 us: cache_step(): v_blk = lax.ppermute(v_blk, SEQ_AXES, perm_next)]
    all_to_all x0 -> x1, blocking collectives: none -> 29.1 us  [local_fn(): o = lax.all_to_all(o, 'sp', split_axis=0, concat_axis=1, tiled=True)]
  transfers between devices with their start and end apart: 16 -> 6, of which waited for: 7 -> 4; matrix products, arithmetic and copies ran while one was open for 41% -> 4% of each run, Pallas kernels for 0% -> 16%
where the time goes in v1:
time: 672 us; the launch traced here: 670 us
  Pallas kernels  441 us (66%)
  waiting for transfers between devices  137 us (20%)
  local copies, waits for them, and re-layouts  31.9 us (5%)
  blocking collectives  29.1 us (4%)
  starting transfers between devices  15.8 us (2%)
  between operations  14.2 us (2%)
    pallas_call x1, Pallas kernels, attention(): pl.pallas_call(functools.partial(attn_kernel, tok=tok, group=group, kblk=...  317 us
    pallas_call x4, Pallas kernels, matmul(): pl.pallas_call(functools.partial(mm_kernel, rope=rope, trans=trans), grid...  123 us
    all_gather x1, waiting for transfers between devices, local_fn(): x_g = lax.all_gather(x_loc, 'cp', axis=0, tiled=True)  59.5 us
    all_gather x1, waiting for transfers between devices, local_fn(): o_g = lax.all_gather(o, 'cp', axis=1, tiled=True)  52.4 us
    all_to_all x1, blocking collectives, local_fn(): o = lax.all_to_all(o, 'sp', split_axis=0, concat_axis=1, tiled=True)  29.1 us
    all_to_all x1, waiting for transfers between devices, local_fn(): y_loc = lax.all_to_all(y, 'cp', split_axis=0, concat_axis=1, tiled=True)  22.1 us
    unnamed x7, local copies, waits for them, and re-layouts  20.3 us
  transfers between devices with their start and end apart: 6, of which 4 were waited for; matrix products, arithmetic and copies ran while one was open for 4% of the time, Pallas kernels for 16%

profile of v1, /device:TPU:0, one launch (start us, length us, event | category | flops | bytes accessed | tf_op | source)
XLA Modules:
  0.0 669.8 jit_solution(13417504372473046022)
XLA Ops:
  7.2 0.0 all-gather.3.cloned.1.call-start
  7.2 0.7 all-gather.3.cloned.1.call-update
  7.9 0.5 fusion
  8.5 0.1 pad_maximum_fusion.1
  8.6 59.5 %all-gather.3.cloned.1.call-done.x_ref = bf16[256,16384]{1,0:T(8,128)(2,1)} async-done(((bf16[64,16384]{1,0:T(8,128)(2,1)}), bf16[256,16384]{1,0:T(8,128)(2,1)}) %all-gather.3.cloned.1.call-update) | async-done | bytes 8388624 | tf_op jit(solution)/shard_map/all_gather | solution.py:207
  68.1 8.1 %shard_map.96 = bf16[256,256]{1,0:T(8,128)(2,1)S(1)} custom-call(s32[1]{0:T(128)} %bitcast.5.off_ref, bf16[256,16384]{1,0:T(8,128)(2,1)} %all-gather.3.cloned.1.call-done.x_ref, bf16[16384,1024]{1,0:T(8,128)(2,1)} %w_ref.6, f32[256,128]{1,0:T(8,128)S(1)} %get-tuple-element.10.cos_ref, f32[256,128]{1,0:T(8,128)S(1)} %get-tuple-element.11.sin_ref), custom_call_target="tpu_custom_call" | custom-call | flops 2147483648 | bytes 8388608 | tf_op jit(solution)/shard_map/pallas_call | solution.py:40
  76.2 8.2 %shard_map.95 = bf16[256,256]{1,0:T(8,128)(2,1)S(1)} custom-call(s32[1]{0:T(128)} %bitcast.5.off_ref, bf16[256,16384]{1,0:T(8,128)(2,1)} %all-gather.3.cloned.1.call-done.x_ref, bf16[16384,1024]{1,0:T(8,128)(2,1)} %w_ref.5, f32[256,128]{1,0:T(8,128)S(1)} %get-tuple-element.10.cos_ref, f32[256,128]{1,0:T(8,128)S(1)} %get-tuple-element.11.sin_ref), custom_call_target="tpu_custom_call" | custom-call | flops 2147483648 | bytes 8388608 | tf_op jit(solution)/shard_map/pallas_call | solution.py:40
  84.4 0.0 copy-start
  84.4 0.9 copy.22
  85.3 4.1 all-to-all-start.1
  89.4 54.2 %shard_map.94 = bf16[4096,256]{1,0:T(8,128)(2,1)} custom-call(s32[1]{0:T(128)} %bitcast.off_ref, bf16[256,16384]{1,0:T(8,128)(2,1)} %all-gather.3.cloned.1.call-done.x_ref, bf16[16384,16384]{1,0:T(8,128)(2,1)} %w_ref.4, f32[256,128]{1,0:T(8,128)S(1)} %get-tuple-element.10.cos_ref, f32[256,128]{1,0:T(8,128)S(1)} %get-tuple-element.11.sin_ref), custom_call_target="tpu_custom_call" | custom-call | flops 34359738368 | bytes 134217728 | tf_op jit(solution)/shard_map/pallas_call | solution.py:40
  143.6 0.0 copy-done
  143.6 0.0 all-to-all-done.1
  143.6 3.8 all-to-all-start
  147.4 0.2 all-gather.5.cloned.1.call-start
  147.6 7.7 %copy.36 = bf16[4096,8,128]{2,0,1:T(8,128)(2,1)} copy(bf16[4096,8,128]{2,1,0:T(8,128)(2,1)} %param.8) | data formatting | bytes 16777216 | tf_op args[1]
  155.3 11.9 %copy.20 = bf16[4096,8,128]{0,2,1:T(8,128)(2,1)} copy(bf16[4096,8,128]{2,1,0:T(8,128)(2,1)} %param.9) | data formatting | bytes 16777216 | tf_op args[2]
  167.2 1.2 copy.37
  168.4 0.2 fusion.2
  168.6 0.7 copy.33
  169.3 0.8 copy.24
  170.1 2.6 all-to-all-done
  172.7 1.5 copy.30
  174.2 317.3 %shard_map.97 = bf16[512,2048]{1,0:T(8,128)(2,1)} custom-call(bf16[8,4096,128]{2,1,0:T(8,128)(2,1)} %bitcast.37, bf16[8,128,4096]{2,1,0:T(8,128)(2,1)} %bitcast.38, bf16[2048,512]{1,0:T(8,128)(2,1)} %bitcast.43, bf16[512,128]{1,0:T(8,128)(2,1)} %bitcast.49, bf16[128,512]{1,0:T(8,128)(2,1)} %bitcast.48), custom_call_target="tpu_custom_call" | custom-call | tf_op jit(solution)/shard_map/pallas_call | solution.py:177
  491.5 0.0 copy-start.1
  491.5 29.1 %all_to_all.87 = bf16[2,256,2048]{2,1,0:T(8,128)(2,1)S(1)} all-to-all(bf16[2,256,2048]{2,1,0:T(8,128)(2,1)} %bitcast.44), channel_id=1, replica_groups=mesh['dp'=1,'sp'=2,'cp'=4] {'sp'}, dimensions={0} | all-to-all | bytes 4194304 | tf_op jit(solution)/shard_map/all_to_all | solution.py:225
  520.6 1.5 copy.31
  522.1 0.0 all-gather.5.cloned.1.call-update
  522.1 0.0 copy-done.1
  522.1 1.0 copy.27
  523.1 4.0 all-to-all-start.4
  527.2 52.4 %all-gather.5.cloned.1.call-done.x_ref = bf16[256,16384]{1,0:T(8,128)(2,1)} async-done(((bf16[256,4096]{1,0:T(8,128)(2,1)}), bf16[256,16384]{1,0:T(8,128)(2,1)}) %all-gather.5.cloned.1.call-update) | async-done | bytes 8388624 | tf_op jit(solution)/shard_map/all_gather | solution.py:226
  579.5 52.9 %shard_map.98 = bf16[256,4096]{1,0:T(8,128)(2,1)} custom-call(s32[1]{0:T(128)} %bitcast.off_ref, bf16[256,16384]{1,0:T(8,128)(2,1)} %all-gather.5.cloned.1.call-done.x_ref, bf16[16384,16384]{1,0:T(8,128)(2,1)} %w_ref.7, f32[256,128]{1,0:T(8,128)S(1)} %get-tuple-element.10.cos_ref, f32[256,128]{1,0:T(8,128)S(1)} %get-tuple-element.11.sin_ref), custom_call_target="tpu_custom_call" | custom-call | flops 34359738368 | bytes 134217728 | tf_op jit(solution)/shard_map/pallas_call | solution.py:40
  632.4 0.0 all-to-all-done.4
  632.4 3.6 all-to-all-start.3
  636.1 1.5 fusion.1
  637.6 0.2 copy.29
  637.7 0.7 reshape_squeeze.7
  638.5 0.2 copy.28
  638.6 0.7 reshape_squeeze.6
  639.3 22.1 %all-to-all-done.3 = bf16[4,64,4096]{2,1,0:T(8,128)(2,1)S(1)} async-done(((bf16[4,64,4096]{2,1,0:T(8,128)(2,1)}), bf16[4,64,4096]{2,1,0:T(8,128)(2,1)S(1)}, u32[]{:S(2)}, u32[]{:S(2)}) %all-to-all-start.3) | async-done | bytes 2097184 | tf_op jit(solution)/shard_map/all_to_all | solution.py:228
  661.5 1.5 copy.32
  (3 shorter events, 0.0 us)
Async XLA Ops:
  7.2 60.9 %all-gather.3.cloned.1.call-start = ((), (), s32[]{:S(2)}) async-start(), calls=%async_computation.5 | async-start | bytes 10485760 | tf_op jit(solution)/shard_map/all_gather | solution.py:207
  84.4 59.2 %copy-start = (bf16[2,256,256]{2,1,0:T(8,128)(2,1)}, bf16[2,256,256]{2,1,0:T(8,128)(2,1)S(1)}, u32[]{:S(2)}) copy-start(bf16[2,256,256]{2,1,0:T(8,128)(2,1)S(1)} %pad_maximum_fusion) | copy-start | bytes 786436
  85.3 58.4 %all-to-all-start.1 = ((bf16[2,256,256]{1,0,2:T(2,128)(2,1)}), bf16[2,256,256]{1,0,2:T(2,128)(2,1)}, u32[]{:S(2)}, u32[]{:S(2)}) async-start(bf16[2,256,256]{1,0,2:T(2,128)(2,1)} %copy.22), calls=%async_computation.1 | async-start | bytes 524288 | tf_op jit(solution)/shard_map/all_to_all | solution.py:222
  143.6 29.1 %all-to-all-start = ((bf16[2,2048,256]{2,1,0:T(8,128)(2,1)}), bf16[2,2048,256]{2,1,0:T(8,128)(2,1)S(1)}, u32[]{:S(2)}, u32[]{:S(2)}) async-start(bf16[2,2048,256]{2,1,0:T(8,128)(2,1)} %bitcast.3), calls=%async_computation | async-start | bytes 4194304 | tf_op jit(solution)/shard_map/all_to_all | solution.py:223
  147.4 432.1 %all-gather.5.cloned.1.call-start = ((), (), s32[]{:S(2)}) async-start(), calls=%async_computation.6 | async-start | bytes 10485760 | tf_op jit(solution)/shard_map/all_gather | solution.py:226
  491.5 30.6 %copy-start.1 = (bf16[2,256,256]{2,1,0:T(8,128)(2,1)S(1)}, bf16[2,256,256]{2,1,0:T(8,128)(2,1)}, u32[]{:S(2)}) copy-start(bf16[2,256,256]{2,1,0:T(8,128)(2,1)} %copy-done) | copy-start | bytes 786436
  523.1 109.3 %all-to-all-start.4 = ((bf16[2,256,256]{2,0,1:T(2,128)(2,1)}), bf16[2,256,256]{2,0,1:T(2,128)(2,1)}, u32[]{:S(2)}, u32[]{:S(2)}) async-start(bf16[2,256,256]{2,0,1:T(2,128)(2,1)} %copy.27), calls=%async_computation.4 | async-start | bytes 524288 | tf_op jit(solution)/shard_map/all_to_all | solution.py:219
  632.4 29.0 %all-to-all-start.3 = ((bf16[4,64,4096]{2,1,0:T(8,128)(2,1)}), bf16[4,64,4096]{2,1,0:T(8,128)(2,1)S(1)}, u32[]{:S(2)}, u32[]{:S(2)}) async-start(bf16[4,64,4096]{2,1,0:T(8,128)(2,1)} %bitcast.14), calls=%async_computation.3 | async-start | bytes 4194304 | tf_op jit(solution)/shard_map/all_to_all | solution.py:228
Sparse Core Ops, SparseCore 0:
  9.5 58.5 all-gather.2
  522.2 57.2 all-gather.4

commit v2 on v1

--- a/solution.py
+++ b/solution.py
@@ -8,6 +8,8 @@
 
 ROPE_BASE = 500000
 HD = 128
+BN_Q = 256
+BN_O = 256
 LOG2E = 1.4426950408889634
 FLIPS = ((0, 0, 0), (0, 0, 1), (0, 1, 0), (1, 0, 0), (0, 1, 1), (1, 0, 1), (1, 1, 0), (1, 1, 1))
 
@@ -56,13 +58,17 @@
     )(off, x, w, cos_t, sin_t)
 
 
-def attn_kernel(kh_ref, vh_ref, qt_ref, kn_ref, vn_ref, o_ref,
-                kb, vb, sbuf, acc, mst, lst, ksend, krecv, vsend, vrecv, *, tok, group, kblk, scale):
+def attn_kernel(kh_ref, vh_ref, qt_ref, kn_ref, vn_ref, og_ref,
+                kb, vb, sbuf, acc, mst, lst, ost, ksend, krecv, vsend, vrecv,
+                osend, orecv, fsend, frecv, *, tok, group, kblk, scale):
     cache = kb.shape[1]
     nsub = cache // kblk
+    half = tok // 2
+    width = group * HD
     sp, cp = lax.axis_index('sp'), lax.axis_index('cp')
     chip, core = cp // 2, cp % 2
     cexp = scale * LOG2E
+    own = 2 * cp + sp
 
     def flip(v, f):
         return 1 - v if f else v
@@ -75,10 +81,13 @@
         s, c = partner(p)
         return {'sp': s, 'cp': c}
 
+    def head_of(p):
+        s, c = partner(p)
+        return 2 * c + s
+
     barrier = pltpu.get_barrier_semaphore()
     for p in range(1, 8):
         pl.semaphore_signal(barrier, inc=1, device_id=dev(p), device_id_type=pl.DeviceIdType.MESH)
-    own = 2 * cp + sp
     k0 = pltpu.make_async_copy(kh_ref.at[own], kb.at[0], krecv.at[0])
     v0 = pltpu.make_async_copy(vh_ref.at[own], vb.at[0], vrecv.at[0])
     k0.start()
@@ -86,11 +95,9 @@
     pl.semaphore_wait(barrier, 7)
 
     def remote(p):
-        s, c = partner(p)
-        head = 2 * c + s
-        ck = pltpu.make_async_remote_copy(kh_ref.at[head], kb.at[p], ksend.at[p], krecv.at[p],
+        ck = pltpu.make_async_remote_copy(kh_ref.at[head_of(p)], kb.at[p], ksend.at[p], krecv.at[p],
                                           device_id=dev(p), device_id_type=pl.DeviceIdType.MESH)
-        cv = pltpu.make_async_remote_copy(vh_ref.at[head], vb.at[p], vsend.at[p], vrecv.at[p],
+        cv = pltpu.make_async_remote_copy(vh_ref.at[head_of(p)], vb.at[p], vsend.at[p], vrecv.at[p],
                                           device_id=dev(p), device_id_type=pl.DeviceIdType.MESH)
         return ck, cv
 
@@ -118,14 +125,30 @@
     lax.fori_loop(0, group, first, 0)
 
     def scores(slot, j, h, dst):
-        keys = kb[slot, pl.ds(j * kblk, kblk), :]
-        sbuf[dst] = jnp.dot(keys, q_of(h), preferred_element_type=jnp.float32)
+        s = jnp.dot(kb[slot, pl.ds(j * kblk, kblk), :], q_of(h), preferred_element_type=jnp.float32)
+        sbuf[dst] = s
+        return jnp.max(s.reshape(kblk // 8, 8, tok), axis=0)
+
+    def out_copies(h):
+        cols = pl.ds(pl.multiple_of(h * HD, HD), HD)
+        dcols = pl.ds(pl.multiple_of(own * width + h * HD, HD), HD)
+        res = [pltpu.make_async_copy(ost.at[pl.ds(sp * half, half), cols], og_ref.at[:, dcols], osend.at[0])]
+        for p in (1, 2, 3, 6):
+            g = flip(sp, FLIPS[p][0])
+            res.append(pltpu.make_async_remote_copy(
+                ost.at[pl.ds(g * half, half), cols], og_ref.at[:, dcols], osend.at[p], orecv.at[p],
+                device_id=dev(p), device_id_type=pl.DeviceIdType.MESH))
+        return res
+
+    def send_out(h):
+        for c in out_copies(h):
+            c.start()
 
     k0.wait()
     v0.wait()
-    scores(0, 0, 0, 0)
-
-    def step(i, carry):
+    m_first = scores(0, 0, 0, 0)
+
+    def step(i, m_ahead):
         slot, h = i // group, i % group
         nxt = jnp.minimum(i + 1, 8 * group - 1)
         nslot, nh = nxt // group, nxt % group
@@ -134,19 +157,23 @@
         def _():
             pltpu.make_async_copy(kb.at[nslot], kb.at[nslot], krecv.at[nslot]).wait()
             pltpu.make_async_copy(vb.at[nslot], vb.at[nslot], vrecv.at[nslot]).wait()
+
+        @pl.when((slot == 7) & (h > 0))
+        def _():
+            send_out(h - 1)
 
         m_run = mst[h, 0:1, :]
         l_run = lst[h]
         o_run = acc[h]
         for j in range(nsub):
+            m_blk = m_ahead
             if j + 1 < nsub:
-                scores(slot, j + 1, h, (j + 1) % 2)
+                m_ahead = scores(slot, j + 1, h, (j + 1) % 2)
             else:
-                scores(nslot, 0, nh, (j + 1) % 2)
-            s = sbuf[j % 2]
-            m_new = jnp.maximum(m_run, jnp.max(s, axis=0, keepdims=True))
+                m_ahead = scores(nslot, 0, nh, (j + 1) % 2)
+            m_new = jnp.maximum(m_run, jnp.max(m_blk, axis=0, keepdims=True))
             alpha = jnp.exp2((m_run - m_new) * cexp)
-            p = jnp.exp2((s - m_new) * cexp)
+            p = jnp.exp2((sbuf[j % 2] - m_new) * cexp)
             l_run = l_run * alpha + jnp.sum(p.reshape(kblk // 8, 8, tok), axis=0)
             o_run = o_run * alpha + jnp.dot(vb[slot, :, pl.ds(j * kblk, kblk)], p.astype(jnp.bfloat16),
                                             preferred_element_type=jnp.float32)
@@ -154,31 +181,46 @@
         mst[h] = jnp.broadcast_to(m_run, (8, tok))
         lst[h] = l_run
         acc[h] = o_run
-        return carry
-
-    lax.fori_loop(0, 8 * group, step, 0)
-
-    def last(h, carry):
-        total = jnp.sum(lst[h], axis=0, keepdims=True)
-        o = acc[h] / total
-        o_ref[:, pl.ds(pl.multiple_of(h * HD, HD), HD)] = o.T.astype(jnp.bfloat16)
-        return carry
-
-    lax.fori_loop(0, group, last, 0)
+
+        @pl.when(slot == 7)
+        def _():
+            o = acc[h] / jnp.sum(lst[h], axis=0, keepdims=True)
+            ost[:, pl.ds(pl.multiple_of(h * HD, HD), HD)] = o.T.astype(jnp.bfloat16)
+
+        return m_ahead
+
+    lax.fori_loop(0, 8 * group, step, m_first)
     for p in range(1, 8):
         ck, cv = remote(p)
         ck.wait_send()
         cv.wait_send()
-
-
-def attention(kh, vh, qt, kn, vnt, kblk=512):
+    send_out(group - 1)
+
+    def cols_of(p):
+        return og_ref.at[:, pl.ds(pl.multiple_of(head_of(p) * width, width), width)]
+
+    def forward(n, p):
+        return pltpu.make_async_remote_copy(cols_of(p), cols_of(p), fsend.at[n], frecv.at[n],
+                                            device_id=dev(1), device_id_type=pl.DeviceIdType.MESH)
+
+    for n, p in enumerate((3, 2, 6)):
+        pltpu.make_async_copy(cols_of(p), cols_of(p), orecv.at[p]).wait()
+        forward(n, p).start()
+    pltpu.make_async_copy(cols_of(1), cols_of(1), orecv.at[1]).wait()
+    for p in (0, 1, 2, 3, 6):
+        pltpu.make_async_copy(ost.at[pl.ds(0, half), :], ost.at[pl.ds(0, half), :], osend.at[p]).wait()
+    for n, p in enumerate((3, 2, 6)):
+        forward(n, p).wait()
+
+
+def attention(kh, vh, qt, kn, vnt, kblk=2048):
     n_kv, cache, _ = kh.shape
     group, tok = qt.shape[0] // HD, qt.shape[1]
     return pl.pallas_call(
         functools.partial(attn_kernel, tok=tok, group=group, kblk=kblk, scale=HD ** -0.5),
         in_specs=[pl.BlockSpec(memory_space=pl.ANY), pl.BlockSpec(memory_space=pl.ANY)] + [pl.BlockSpec(memory_space=pltpu.VMEM)] * 3,
-        out_specs=pl.BlockSpec(memory_space=pltpu.VMEM),
-        out_shape=jax.ShapeDtypeStruct((tok, group * HD), jnp.bfloat16),
+        out_specs=pl.BlockSpec(memory_space=pl.ANY),
+        out_shape=jax.ShapeDtypeStruct((tok // 2, n_kv * group * HD), jnp.bfloat16),
         scratch_shapes=[
             pltpu.VMEM((8, cache, HD), jnp.bfloat16),
             pltpu.VMEM((8, HD, cache), jnp.bfloat16),
@@ -186,13 +228,96 @@
             pltpu.VMEM((group, HD, tok), jnp.float32),
             pltpu.VMEM((group, 8, tok), jnp.float32),
             pltpu.VMEM((group, 8, tok), jnp.float32),
-            pltpu.SemaphoreType.DMA((8,)),
-            pltpu.SemaphoreType.DMA((8,)),
-            pltpu.SemaphoreType.DMA((8,)),
-            pltpu.SemaphoreType.DMA((8,)),
+            pltpu.VMEM((tok, group * HD), jnp.bfloat16),
+        ] + [pltpu.SemaphoreType.DMA((8,))] * 6 + [pltpu.SemaphoreType.DMA((3,))] * 2,
+        compiler_params=pltpu.CompilerParams(collective_id=0, has_side_effects=True, vmem_limit_bytes=62 << 20),
+    )(kh, vh, qt, kn, vnt)
+
+
+def oproj_kernel(x_hbm, w_hbm, y_hbm, x_ref, wbuf, yst, xsem, wsem, ysend, yrecv, *, bn, rows):
+    sp, cp = lax.axis_index('sp'), lax.axis_index('cp')
+    chip, core = cp // 2, cp % 2
+    steps = yst.shape[0]
+    base = cp * (steps * bn)
+
+    def dev(f):
+        c = (1 - chip if f // 2 else chip) * 2 + (1 - core if f % 2 else core)
+        return c, {'sp': sp, 'cp': c}
+
+    barrier = pltpu.get_barrier_semaphore()
+    for f in range(1, 4):
+        pl.semaphore_signal(barrier, inc=1, device_id=dev(f)[1], device_id_type=pl.DeviceIdType.MESH)
+
+    def wcopy(n, slot):
+        cols = pl.ds(pl.multiple_of(base + n * bn, bn), bn)
+        return pltpu.make_async_copy(w_hbm.at[:, cols], wbuf.at[slot], wsem.at[slot])
+
+    xc = pltpu.make_async_copy(x_hbm, x_ref, xsem)
+    xc.start()
+    wcopy(0, 0).start()
+    wcopy(1, 1).start()
+    pl.semaphore_wait(barrier, 3)
+    xc.wait()
+
+    def y_copies(n):
+        cols = pl.ds(pl.multiple_of(base + n * bn, bn), bn)
+        res = [pltpu.make_async_copy(yst.at[n, pl.ds(cp * rows, rows), :], y_hbm.at[:, cols], ysend.at[0])]
+        for f in range(1, 4):
+            c, d = dev(f)
+            res.append(pltpu.make_async_remote_copy(yst.at[n, pl.ds(c * rows, rows), :], y_hbm.at[:, cols], ysend.at[f], yrecv.at[f],
+                                                    device_id=d, device_id_type=pl.DeviceIdType.MESH))
+        return res
+
+    def send(n):
+        for c in y_copies(n):
+            c.start()
+
+    def step(n, carry):
+        slot = n % 2
+        wcopy(n, slot).wait()
+        yst[n] = jnp.dot(x_ref[...], wbuf[slot], preferred_element_type=jnp.float32).astype(jnp.bfloat16)
+
+        @pl.when(n + 2 < steps)
+        def _():
+            wcopy(n + 2, slot).start()
+
+        @pl.when(n > 0)
+        def _():
+            send(n - 1)
+
+        return carry
+
+    lax.fori_loop(0, steps, step, 0)
+    send(steps - 1)
+    width = steps * bn
+    for f in range(4):
+        c, _ = dev(f)
+        mine = y_hbm.at[:, pl.ds(pl.multiple_of(c * width, width), width)]
+        pltpu.make_async_copy(mine, mine, ysend.at[f]).wait()
+        if f:
+            pltpu.make_async_copy(mine, mine, yrecv.at[f]).wait()
+
+
+def out_project(o_g, w_o, cp_size, bn=256):
+    rows, depth = o_g.shape
+    n_cols = w_o.shape[1]
+    steps = n_cols // cp_size // bn
+    return pl.pallas_call(
+        functools.partial(oproj_kernel, bn=bn, rows=rows // cp_size),
+        in_specs=[pl.BlockSpec(memory_space=pl.ANY)] * 2,
+        out_specs=pl.BlockSpec(memory_space=pl.ANY),
+        out_shape=jax.ShapeDtypeStruct((rows // cp_size, n_cols), jnp.bfloat16),
+        scratch_shapes=[
+            pltpu.VMEM((rows, depth), jnp.bfloat16),
+            pltpu.VMEM((2, depth, bn), jnp.bfloat16),
+            pltpu.VMEM((steps, rows, bn), jnp.bfloat16),
+            pltpu.SemaphoreType.DMA,
+            pltpu.SemaphoreType.DMA((2,)),
+            pltpu.SemaphoreType.DMA((4,)),
+            pltpu.SemaphoreType.DMA((4,)),
         ],
-        compiler_params=pltpu.CompilerParams(collective_id=0, has_side_effects=True, vmem_limit_bytes=60 << 20),
-    )(kh, vh, qt, kn, vnt)
+        compiler_params=pltpu.CompilerParams(collective_id=1, has_side_effects=True, vmem_limit_bytes=60 << 20),
+    )(o_g, w_o)
 
 
 def solution(mesh):
@@ -208,24 +333,22 @@
         cos_t, sin_t = rope_tables(cache_loc * seq_size + sp * rows + jnp.arange(rows))
         kh = jnp.transpose(kc_loc, (1, 0, 2))
         vh = jnp.transpose(vc_loc, (1, 2, 0))
+        x_g, kh, vh = lax.optimization_barrier((x_g, kh, vh))
         q_cols = w_q.shape[1] // cp_size
         k_cols = w_k.shape[1] // cp_size
-        qoff = jnp.reshape(cp * (q_cols // 256), (1,)).astype(jnp.int32)
+        qoff = jnp.reshape(cp * (q_cols // BN_Q), (1,)).astype(jnp.int32)
         koff = jnp.reshape(cp * (k_cols // 256), (1,)).astype(jnp.int32)
         k_part = matmul(x_g, w_k, cos_t, sin_t, koff, k_cols, rope=True)
         v_part = matmul(x_g, w_v, cos_t, sin_t, koff, k_cols, rope=False)
-        qt = matmul(x_g, w_q, cos_t, sin_t, qoff, q_cols, rope=True, trans=True)
+        qt = matmul(x_g, w_q, cos_t, sin_t, qoff, q_cols, rope=True, trans=True, bn=BN_Q)
         kv = jnp.stack([k_part, v_part], 0)
         kv_rows = lax.all_to_all(kv, 'cp', split_axis=1, concat_axis=2, tiled=True)
         k_new = kv_rows[0].reshape(x_loc.shape[0], n_kv, HD)
         v_new = kv_rows[1].reshape(x_loc.shape[0], n_kv, HD)
         kv_head = lax.all_to_all(kv, 'sp', split_axis=2, concat_axis=1, tiled=True)
         qt = lax.all_to_all(qt, 'sp', split_axis=0, concat_axis=1, tiled=True)
-        o = attention(kh, vh, qt, kv_head[0], kv_head[1].T)
-        o = lax.all_to_all(o, 'sp', split_axis=0, concat_axis=1, tiled=True)
-        o_g = lax.all_gather(o, 'cp', axis=1, tiled=True)
-        y = matmul(o_g, w_o, cos_t, sin_t, qoff, q_cols, rope=False)
-        y_loc = lax.all_to_all(y, 'cp', split_axis=0, concat_axis=1, tiled=True)
+        o_g = attention(kh, vh, qt, kv_head[0], kv_head[1].T)
+        y_loc = out_project(o_g, w_o, cp_size, BN_O)
         return y_loc, k_new, v_new
 
     return jax.shard_map(local_fn, mesh=mesh, in_specs=(row_spec, row_spec, row_spec, P(), P(), P(), P()), out_specs=(row_spec, row_spec, row_spec), check_vma=False)

time: 672 us -> 569 us (0.85)
  waiting for transfers between devices: 137 us -> 64.4 us
  blocking collectives: 29.1 us -> 0 us
    pallas_call x0 -> x1, Pallas kernels: none -> 54.1 us  [out_project(): pl.pallas_call(functools.partial(oproj_kernel, bn=bn, rows=rows // cp_siz...]
    pallas_call x4 -> x3, Pallas kernels: 123 us -> 70.5 us  [matmul(): pl.pallas_call(functools.partial(mm_kernel, rope=rope, trans=trans), grid...]
    all_gather x1 -> x0, waiting for transfers between devices: 52.4 us -> none  [local_fn(): o_g = lax.all_gather(o, 'cp', axis=1, tiled=True)]
    all_to_all x1 -> x0, blocking collectives: 29.1 us -> none  [local_fn(): o = lax.all_to_all(o, 'sp', split_axis=0, concat_axis=1, tiled=True)]
    all_to_all x1 -> x0, waiting for transfers between devices: 22.1 us -> none  [local_fn(): y_loc = lax.all_to_all(y, 'cp', split_axis=0, concat_axis=1, tiled=True)]
    all_gather x1, waiting for transfers between devices: 59.5 us -> 39.9 us  [local_fn(): x_g = lax.all_gather(x_loc, 'cp', axis=0, tiled=True)]
    all_to_all x1, waiting for transfers between devices: 2.63 us -> 19.2 us  [local_fn(): qt = lax.all_to_all(qt, 'sp', split_axis=0, concat_axis=1, tiled=True)]
    unnamed x7 -> x6, local copies, waits for them, and re-layouts: 20.3 us -> 23.3 us
  transfers between devices with their start and end apart: 6 -> 4, of which waited for: 4 -> 3; matrix products, arithmetic and copies ran while one was open for 4% -> 5% of each run, Pallas kernels for 16% -> 10%
where the time goes in v2:
time: 569 us; the launch traced here: 567 us
  Pallas kernels  444 us (78%)
  waiting for transfers between devices  64.4 us (11%)
  local copies, waits for them, and re-layouts  32.1 us (6%)
  between operations  14.1 us (2%)
  starting transfers between devices  11.5 us (2%)
    pallas_call x1, Pallas kernels, attention(): pl.pallas_call(functools.partial(attn_kernel, tok=tok, group=group, kblk=...  320 us
    pallas_call x3, Pallas kernels, matmul(): pl.pallas_call(functools.partial(mm_kernel, rope=rope, trans=trans), grid...  70.5 us
    pallas_call x1, Pallas kernels, out_project(): pl.pallas_call(functools.partial(oproj_kernel, bn=bn, rows=rows // cp_siz...  54.1 us
    all_gather x1, waiting for transfers between devices, local_fn(): x_g = lax.all_gather(x_loc, 'cp', axis=0, tiled=True)  39.9 us
    unnamed x6, local copies, waits for them, and re-layouts  23.3 us
    all_to_all x1, waiting for transfers between devices, local_fn(): qt = lax.all_to_all(qt, 'sp', split_axis=0, concat_axis=1, tiled=True)  19.2 us
  transfers between devices with their start and end apart: 4, of which 3 were waited for; matrix products, arithmetic and copies ran while one was open for 5% of the time, Pallas kernels for 10%

profile of v2, /device:TPU:0, one launch (start us, length us, event | category | flops | bytes accessed | tf_op | source)
XLA Modules:
  0.0 567.2 jit_solution(2414962626582039508)
XLA Ops:
  7.2 0.0 all-gather.2.cloned.1.call-start
  7.2 0.7 all-gather.2.cloned.1.call-update
  7.9 7.7 %copy.30 = bf16[4096,8,128]{2,0,1:T(8,128)(2,1)} copy(bf16[4096,8,128]{2,1,0:T(8,128)(2,1)} %param.8) | data formatting | bytes 16777216 | tf_op args[1]
  15.6 11.9 %copy.18 = bf16[4096,8,128]{0,2,1:T(8,128)(2,1)} copy(bf16[4096,8,128]{2,1,0:T(8,128)(2,1)} %param.9) | data formatting | bytes 16777216 | tf_op args[2]
  27.5 0.5 fusion
  28.0 0.1 pad_maximum_fusion.1
  28.2 39.9 %all-gather.2.cloned.1.call-done.x_ref = bf16[256,16384]{1,0:T(8,128)(2,1)} async-done(((bf16[64,16384]{1,0:T(8,128)(2,1)}), bf16[256,16384]{1,0:T(8,128)(2,1)}) %all-gather.2.cloned.1.call-update) | async-done | bytes 8388624 | tf_op jit(solution)/shard_map/all_gather | solution.py:332
  68.1 8.1 %shard_map.96 = bf16[256,256]{1,0:T(8,128)(2,1)S(1)} custom-call(s32[1]{0:T(128)} %bitcast.5.off_ref, bf16[256,16384]{1,0:T(8,128)(2,1)} %all-gather.2.cloned.1.call-done.x_ref, bf16[16384,1024]{1,0:T(8,128)(2,1)} %w_ref.5, f32[256,128]{1,0:T(8,128)S(1)} %get-tuple-element.16.cos_ref, f32[256,128]{1,0:T(8,128)S(1)} %get-tuple-element.17.sin_ref), custom_call_target="tpu_custom_call" | custom-call | flops 2147483648 | bytes 8388608 | tf_op jit(solution)/shard_map/pallas_call | solution.py:42
  76.2 8.2 %shard_map.95 = bf16[256,256]{1,0:T(8,128)(2,1)S(1)} custom-call(s32[1]{0:T(128)} %bitcast.5.off_ref, bf16[256,16384]{1,0:T(8,128)(2,1)} %all-gather.2.cloned.1.call-done.x_ref, bf16[16384,1024]{1,0:T(8,128)(2,1)} %w_ref.4, f32[256,128]{1,0:T(8,128)S(1)} %get-tuple-element.16.cos_ref, f32[256,128]{1,0:T(8,128)S(1)} %get-tuple-element.17.sin_ref), custom_call_target="tpu_custom_call" | custom-call | flops 2147483648 | bytes 8388608 | tf_op jit(solution)/shard_map/pallas_call | solution.py:42
  84.4 0.9 copy.20
  85.3 3.4 all-to-all-start.1
  88.7 1.0 copy.23
  89.7 4.6 all-to-all-done.1
  94.3 0.0 copy-start
  94.3 4.0 all-to-all-start.2
  98.4 54.2 %shard_map.94 = bf16[4096,256]{1,0:T(8,128)(2,1)} custom-call(s32[1]{0:T(128)} %bitcast.2.off_ref, bf16[256,16384]{1,0:T(8,128)(2,1)} %all-gather.2.cloned.1.call-done.x_ref, bf16[16384,16384]{1,0:T(8,128)(2,1)} %w_ref.3, f32[256,128]{1,0:T(8,128)S(1)} %get-tuple-element.16.cos_ref, f32[256,128]{1,0:T(8,128)S(1)} %get-tuple-element.17.sin_ref), custom_call_target="tpu_custom_call" | custom-call | flops 34359738368 | bytes 134217728 | tf_op jit(solution)/shard_map/pallas_call | solution.py:42
  152.6 0.0 copy-done
  152.6 0.0 all-to-all-done.2
  152.6 4.0 all-to-all-start
  156.6 1.2 copy.31
  157.8 0.2 fusion.2
  158.0 0.7 copy.27
  158.7 0.8 copy.22
  159.5 1.5 fusion.1
  161.0 0.2 copy.25
  161.1 0.7 reshape_squeeze.7
  161.8 0.2 copy.24
  162.0 0.7 reshape_squeeze.6
  162.7 19.2 %all-to-all-done = bf16[2,2048,256]{2,1,0:T(8,128)(2,1)S(1)} async-done(((bf16[2,2048,256]{2,1,0:T(8,128)(2,1)}), bf16[2,2048,256]{2,1,0:T(8,128)(2,1)S(1)}, u32[]{:S(2)}, u32[]{:S(2)}) %all-to-all-start) | async-done | bytes 2097184 | tf_op jit(solution)/shard_map/all_to_all | solution.py:349
  181.9 1.5 copy.26
  183.4 319.8 %shard_map.97.x_hbm = bf16[256,16384]{1,0:T(8,128)(2,1)} custom-call(bf16[8,4096,128]{2,1,0:T(8,128)(2,1)} %bitcast.29, bf16[8,128,4096]{2,1,0:T(8,128)(2,1)} %bitcast.30, bf16[2048,512]{1,0:T(8,128)(2,1)} %bitcast.32, bf16[512,128]{1,0:T(8,128)(2,1)} %bitcast.36, bf16[128,512]{1,0:T(8,128)(2,1)} %bitcast.35), custom_call_target="tpu_custom_call" | custom-call | tf_op jit(solution)/shard_map/pallas_call | solution.py:219
  503.2 54.1 %shard_map.98 = bf16[64,16384]{1,0:T(8,128)(2,1)} custom-call(bf16[256,16384]{1,0:T(8,128)(2,1)} %shard_map.97.x_hbm, bf16[16384,16384]{1,0:T(8,128)(2,1)} %w_hbm.1), custom_call_target="tpu_custom_call" | custom-call | tf_op jit(solution)/shard_map/pallas_call | solution.py:305
  557.3 3.0 copy.33
  (3 shorter events, 0.0 us)
Async XLA Ops:
  7.2 60.9 %all-gather.2.cloned.1.call-start = ((), (), s32[]{:S(2)}) async-start(), calls=%async_computation.3 | async-start | bytes 10485760 | tf_op jit(solution)/shard_map/all_gather | solution.py:332
  85.3 9.1 %all-to-all-start.1 = ((bf16[2,256,256]{1,0,2:T(2,128)(2,1)}), bf16[2,256,256]{1,0,2:T(2,128)(2,1)S(1)}, u32[]{:S(2)}, u32[]{:S(2)}) async-start(bf16[2,256,256]{1,0,2:T(2,128)(2,1)} %copy.20), calls=%async_computation.1 | async-start | bytes 524288 | tf_op jit(solution)/shard_map/all_to_all | solution.py:348
  94.3 58.3 %copy-start = (bf16[2,256,256]{1,0,2:T(2,128)(2,1)}, bf16[2,256,256]{1,0,2:T(2,128)(2,1)S(1)}, u32[]{:S(2)}) copy-start(bf16[2,256,256]{1,0,2:T(2,128)(2,1)S(1)} %all-to-all-done.1) | copy-start | bytes 786436
  94.3 58.3 %all-to-all-start.2 = ((bf16[2,256,256]{2,0,1:T(2,128)(2,1)}), bf16[2,256,256]{2,0,1:T(2,128)(2,1)}, u32[]{:S(2)}, u32[]{:S(2)}) async-start(bf16[2,256,256]{2,0,1:T(2,128)(2,1)} %copy.23), calls=%async_computation.2 | async-start | bytes 524288 | tf_op jit(solution)/shard_map/all_to_all | solution.py:345
  152.6 29.3 %all-to-all-start = ((bf16[2,2048,256]{2,1,0:T(8,128)(2,1)}), bf16[2,2048,256]{2,1,0:T(8,128)(2,1)S(1)}, u32[]{:S(2)}, u32[]{:S(2)}) async-start(bf16[2,2048,256]{2,1,0:T(8,128)(2,1)} %bitcast.3), calls=%async_computation | async-start | bytes 4194304 | tf_op jit(solution)/shard_map/all_to_all | solution.py:349
Sparse Core Ops, SparseCore 0:
  9.5 58.5 all-gather.1

commit v3 on v2

--- a/solution.py
+++ b/solution.py
@@ -8,7 +8,6 @@
 
 ROPE_BASE = 500000
 HD = 128
-BN_Q = 256
 BN_O = 256
 LOG2E = 1.4426950408889634
 FLIPS = ((0, 0, 0), (0, 0, 1), (0, 1, 0), (1, 0, 0), (0, 1, 1), (1, 0, 1), (1, 1, 0), (1, 1, 1))
@@ -21,41 +20,171 @@
     return jnp.concatenate([cos_t, cos_t], 1), jnp.concatenate([-sin_t, sin_t], 1)
 
 
-def mm_kernel(off_ref, x_ref, w_ref, cos_ref, sin_ref, o_ref, *, rope, trans):
-    acc = jnp.dot(x_ref[...], w_ref[...], preferred_element_type=jnp.float32).astype(jnp.bfloat16)
-    if not rope:
-        o_ref[...] = acc
-        return
-    for h in range(acc.shape[1] // HD):
-        part = acc[:, h * HD:(h + 1) * HD].astype(jnp.float32)
-        part = part * cos_ref[...] + pltpu.roll(part, HD // 2, 1) * sin_ref[...]
-        if trans:
-            o_ref[h * HD:(h + 1) * HD, :] = part.T.astype(jnp.bfloat16)
-        else:
-            o_ref[:, h * HD:(h + 1) * HD] = part.astype(jnp.bfloat16)
-
-
-def matmul(x, w, cos_t, sin_t, off, n_cols, *, rope, trans=False, bn=256):
-    rows, depth = x.shape
-    out = (n_cols, rows) if trans else (rows, n_cols)
-    ospec = pl.BlockSpec((bn, rows), lambda n, o: (n, 0)) if trans else pl.BlockSpec((rows, bn), lambda n, o: (0, n))
+def front_kernel(x_hbm, wq_hbm, wk_hbm, wv_hbm, cos_ref, sin_ref, qt_ref, kvr_hbm, kvh_hbm,
+                 xg, wbuf, kvbuf, acc, kvacc, kvst, xsem, wsem, kvsem, xsend, xcore, xchip, fsend, frecv,
+                 ssend, srecv, *, kblk, chunk):
+    sp, cp = lax.axis_index('sp'), lax.axis_index('cp')
+    chip, core = cp // 2, cp % 2
+    rows, depth = x_hbm.shape
+    n_cols = acc.shape[1]
+    kv_cols = kvst.shape[2]
+    steps, chunks = depth // kblk, depth // chunk
+    per = chunk // kblk
+    n_buf = wbuf.shape[0]
+
+    def peer(f):
+        return (1 - chip if f // 2 else chip) * 2 + (1 - core if f % 2 else core)
+
+    def dev(f):
+        return {'sp': sp, 'cp': peer(f)}
+
+    other = {'sp': 1 - sp, 'cp': cp}
+    barrier = pltpu.get_barrier_semaphore()
+    for d in (dev(1), dev(2), dev(3), other):
+        pl.semaphore_signal(barrier, inc=1, device_id=d, device_id_type=pl.DeviceIdType.MESH)
+
+    def w_copies(k):
+        slot = k % n_buf
+        depth_k = pl.ds(pl.multiple_of(k * kblk, kblk), kblk)
+        kv_c = pl.ds(pl.multiple_of(cp * kv_cols, kv_cols), kv_cols)
+        return (pltpu.make_async_copy(wq_hbm.at[depth_k, pl.ds(pl.multiple_of(cp * n_cols, n_cols), n_cols)], wbuf.at[slot], wsem.at[slot]),
+                pltpu.make_async_copy(wk_hbm.at[depth_k, kv_c], kvbuf.at[slot, 0], kvsem.at[slot, 0]),
+                pltpu.make_async_copy(wv_hbm.at[depth_k, kv_c], kvbuf.at[slot, 1], kvsem.at[slot, 1]))
+
+    def part(f, c):
+        return pl.ds(pl.multiple_of(peer(f) * rows, rows), rows), pl.ds(pl.multiple_of(c * chunk, chunk), chunk)
+
+    mine = xg.at[pl.ds(pl.multiple_of(cp * rows, rows), rows), :]
+    local = pltpu.make_async_copy(x_hbm, mine, xsem)
+    local.start()
+    for k in range(n_buf - 1):
+        for c in w_copies(k):
+            c.start()
+    pl.semaphore_wait(barrier, 4)
+
+    def to_chip(c):
+        return pltpu.make_async_remote_copy(x_hbm.at[:, part(0, c)[1]], xg.at[part(0, c)], xsend.at[0, c], xchip.at[c],
+                                            device_id=dev(2), device_id_type=pl.DeviceIdType.MESH)
+
+    def to_core(c):
+        return pltpu.make_async_remote_copy(x_hbm.at[:, part(0, c)[1]], xg.at[part(0, c)], xsend.at[1, c], xcore.at[c],
+                                            device_id=dev(1), device_id_type=pl.DeviceIdType.MESH)
+
+    def forward(c):
+        return pltpu.make_async_remote_copy(xg.at[part(2, c)], xg.at[part(2, c)], fsend.at[c], frecv.at[c],
+                                            device_id=dev(1), device_id_type=pl.DeviceIdType.MESH)
+
+    def arrived(f, c, sem):
+        pltpu.make_async_copy(xg.at[part(f, c)], xg.at[part(f, c)], sem.at[c]).wait()
+
+    for c in range(chunks):
+        to_chip(c).start()
+        to_core(c).start()
+    acc[...] = jnp.zeros_like(acc)
+    kvacc[...] = jnp.zeros_like(kvacc)
+    local.wait()
+    arrived(2, 0, xchip)
+    forward(0).start()
+
+    def step(k, carry):
+        c = k // per
+
+        @pl.when(k % per == 0)
+        def _():
+            arrived(1, c, xcore)
+            arrived(3, c, frecv)
+
+        slot = k % n_buf
+        for cpy in w_copies(k):
+            cpy.wait()
+
+        @pl.when(k + n_buf - 1 < steps)
+        def _():
+            for cpy in w_copies(k + n_buf - 1):
+                cpy.start()
+
+        xk = xg[:, pl.ds(pl.multiple_of(k * kblk, kblk), kblk)]
+        acc[...] += jnp.dot(xk, wbuf[slot], preferred_element_type=jnp.float32)
+        for n in range(2):
+            kvacc[n] += jnp.dot(xk, kvbuf[slot, n], preferred_element_type=jnp.float32)
+
+        @pl.when((k % per == per // 2) & (c + 1 < chunks))
+        def _():
+            arrived(2, c + 1, xchip)
+            forward(c + 1).start()
+
+        return carry
+
+    lax.fori_loop(0, steps, step, 0)
+
+    def rope(v):
+        v = v.astype(jnp.bfloat16).astype(jnp.float32)
+        return v * cos_ref[...] + pltpu.roll(v, HD // 2, 1) * sin_ref[...]
+
+    for h in range(kv_cols // HD):
+        kvst[0, :, h * HD:(h + 1) * HD] = rope(kvacc[0, :, h * HD:(h + 1) * HD]).astype(jnp.bfloat16)
+    kvst[1] = kvacc[1].astype(jnp.bfloat16)
+
+    def q_head(h, carry):
+        cols = pl.ds(pl.multiple_of(h * HD, HD), HD)
+        qt_ref[cols, :] = rope(acc[:, cols]).T.astype(jnp.bfloat16)
+        return carry
+
+    heads = n_cols // HD
+    lax.fori_loop(0, heads // 2, q_head, 0)
+    all_rows = rows * 4
+    dcols = pl.ds(pl.multiple_of(cp * kv_cols, kv_cols), kv_cols)
+    copies = []
+    for n in range(2):
+        for f in range(4):
+            src = kvst.at[n, pl.ds(pl.multiple_of(peer(f) * rows, rows), rows), :]
+            dst = kvr_hbm.at[n, :, dcols]
+            if f:
+                copies.append(pltpu.make_async_remote_copy(src, dst, ssend.at[n, f], srecv.at[n, f], device_id=dev(f), device_id_type=pl.DeviceIdType.MESH))
+            else:
+                copies.append(pltpu.make_async_copy(src, dst, ssend.at[n, f]))
+        dst = kvh_hbm.at[n, pl.ds(pl.multiple_of(sp * all_rows, all_rows), all_rows), :]
+        src = kvst.at[n, :, pl.ds(pl.multiple_of(sp * HD, HD), HD)]
+        copies.append(pltpu.make_async_copy(src, dst, ssend.at[n, 4]))
+        src = kvst.at[n, :, pl.ds(pl.multiple_of((1 - sp) * HD, HD), HD)]
+        copies.append(pltpu.make_async_remote_copy(src, dst, ssend.at[n, 5], srecv.at[n, 5], device_id=other, device_id_type=pl.DeviceIdType.MESH))
+    for cpy in copies:
+        cpy.start()
+    lax.fori_loop(heads // 2, heads, q_head, 0)
+    for c in range(chunks):
+        to_chip(c).wait_send()
+        to_core(c).wait_send()
+        forward(c).wait_send()
+    for cpy in copies:
+        cpy.wait()
+
+
+def front(x_loc, w_q, w_k, w_v, cos_t, sin_t, cp_size, kblk=512, chunk=2048, n_buf=4):
+    rows, depth = x_loc.shape
+    n_cols, kv_cols = w_q.shape[1] // cp_size, w_k.shape[1] // cp_size
+    chunks = depth // chunk
+    dma = pltpu.SemaphoreType.DMA
     return pl.pallas_call(
-        functools.partial(mm_kernel, rope=rope, trans=trans),
-        grid_spec=pltpu.PrefetchScalarGridSpec(
-            num_scalar_prefetch=1,
-            grid=(n_cols // bn,),
-            in_specs=[
-                pl.BlockSpec((rows, depth), lambda n, o: (0, 0), pipeline_mode=pl.Buffered(1)),
-                pl.BlockSpec((depth, bn), lambda n, o: (0, o[0] + n)),
-                pl.BlockSpec((rows, HD), lambda n, o: (0, 0)),
-                pl.BlockSpec((rows, HD), lambda n, o: (0, 0)),
-            ],
-            out_specs=ospec,
-        ),
-        out_shape=jax.ShapeDtypeStruct(out, jnp.bfloat16),
-        compiler_params=pltpu.CompilerParams(vmem_limit_bytes=48 << 20),
-        cost_estimate=pl.CostEstimate(flops=2 * rows * depth * n_cols, bytes_accessed=2 * depth * n_cols, transcendentals=0),
-    )(off, x, w, cos_t, sin_t)
+        functools.partial(front_kernel, kblk=kblk, chunk=chunk),
+        in_specs=[pl.BlockSpec(memory_space=pl.ANY)] * 4 + [pl.BlockSpec(memory_space=pltpu.VMEM)] * 2,
+        out_specs=[pl.BlockSpec(memory_space=pltpu.VMEM)] + [pl.BlockSpec(memory_space=pl.ANY)] * 2,
+        out_shape=[
+            jax.ShapeDtypeStruct((n_cols, rows * cp_size), jnp.bfloat16),
+            jax.ShapeDtypeStruct((2, rows, w_k.shape[1]), jnp.bfloat16),
+            jax.ShapeDtypeStruct((2, 2 * rows * cp_size, HD), jnp.bfloat16),
+        ],
+        scratch_shapes=[
+            pltpu.VMEM((rows * cp_size, depth), jnp.bfloat16),
+            pltpu.VMEM((n_buf, kblk, n_cols), jnp.bfloat16),
+            pltpu.VMEM((n_buf, 2, kblk, kv_cols), jnp.bfloat16),
+            pltpu.VMEM((rows * cp_size, n_cols), jnp.float32),
+            pltpu.VMEM((2, rows * cp_size, kv_cols), jnp.float32),
+            pltpu.VMEM((2, rows * cp_size, kv_cols), jnp.bfloat16),
+            dma, dma((n_buf,)), dma((n_buf, 2)), dma((2, chunks)), dma((chunks,)), dma((chunks,)),
+            dma((chunks,)), dma((chunks,)), dma((2, 6)), dma((2, 6)),
+        ],
+        compiler_params=pltpu.CompilerParams(collective_id=2, has_side_effects=True, vmem_limit_bytes=56 << 20),
+    )(x_loc, w_q, w_k, w_v, cos_t, sin_t)
 
 
 def attn_kernel(kh_ref, vh_ref, qt_ref, kn_ref, vn_ref, og_ref,
@@ -122,7 +251,7 @@
         acc[h] = jnp.dot(vn_ref[...], p.astype(jnp.bfloat16), preferred_element_type=jnp.float32)
         return carry
 
-    lax.fori_loop(0, group, first, 0)
+    lax.fori_loop(0, group, first, 0, unroll=2)
 
     def scores(slot, j, h, dst):
         s = jnp.dot(kb[slot, pl.ds(j * kblk, kblk), :], q_of(h), preferred_element_type=jnp.float32)
@@ -148,12 +277,18 @@
     v0.wait()
     m_first = scores(0, 0, 0, 0)
 
+    tail = 6 * group
+
+    def place(i):
+        t = i // tail
+        r = i % tail
+        return (1 - t) * (i // group) + t * (6 + r % 2), (1 - t) * (i % group) + t * (r // 2)
+
     def step(i, m_ahead):
-        slot, h = i // group, i % group
-        nxt = jnp.minimum(i + 1, 8 * group - 1)
-        nslot, nh = nxt // group, nxt % group
-
-        @pl.when((h == group - 1) & (slot < 7))
+        slot, h = place(i)
+        nslot, nh = place(jnp.minimum(i + 1, 8 * group - 1))
+
+        @pl.when(((i % group == group - 1) & (i < tail)) | (i == tail))
         def _():
             pltpu.make_async_copy(kb.at[nslot], kb.at[nslot], krecv.at[nslot]).wait()
             pltpu.make_async_copy(vb.at[nslot], vb.at[nslot], vrecv.at[nslot]).wait()
@@ -237,7 +372,7 @@
 def oproj_kernel(x_hbm, w_hbm, y_hbm, x_ref, wbuf, yst, xsem, wsem, ysend, yrecv, *, bn, rows):
     sp, cp = lax.axis_index('sp'), lax.axis_index('cp')
     chip, core = cp // 2, cp % 2
-    steps = yst.shape[0]
+    steps, n_buf = yst.shape[0], wbuf.shape[0]
     base = cp * (steps * bn)
 
     def dev(f):
@@ -254,8 +389,8 @@
 
     xc = pltpu.make_async_copy(x_hbm, x_ref, xsem)
     xc.start()
-    wcopy(0, 0).start()
-    wcopy(1, 1).start()
+    for n in range(n_buf):
+        wcopy(n, n).start()
     pl.semaphore_wait(barrier, 3)
     xc.wait()
 
@@ -273,13 +408,13 @@
             c.start()
 
     def step(n, carry):
-        slot = n % 2
+        slot = n % n_buf
         wcopy(n, slot).wait()
         yst[n] = jnp.dot(x_ref[...], wbuf[slot], preferred_element_type=jnp.float32).astype(jnp.bfloat16)
 
-        @pl.when(n + 2 < steps)
-        def _():
-            wcopy(n + 2, slot).start()
+        @pl.when(n + n_buf < steps)
+        def _():
+            wcopy(n + n_buf, slot).start()
 
         @pl.when(n > 0)
         def _():
@@ -309,10 +444,10 @@
         out_shape=jax.ShapeDtypeStruct((rows // cp_size, n_cols), jnp.bfloat16),
         scratch_shapes=[
             pltpu.VMEM((rows, depth), jnp.bfloat16),
-            pltpu.VMEM((2, depth, bn), jnp.bfloat16),
+            pltpu.VMEM((4, depth, bn), jnp.bfloat16),
             pltpu.VMEM((steps, rows, bn), jnp.bfloat16),
             pltpu.SemaphoreType.DMA,
-            pltpu.SemaphoreType.DMA((2,)),
+            pltpu.SemaphoreType.DMA((4,)),
             pltpu.SemaphoreType.DMA((4,)),
             pltpu.SemaphoreType.DMA((4,)),
         ],
@@ -327,26 +462,16 @@
     def local_fn(x_loc, kc_loc, vc_loc, w_q, w_k, w_v, w_o):
         cache_loc, n_kv, _ = kc_loc.shape
         seq_size = mesh.shape['sp'] * cp_size
-        sp, cp = lax.axis_index('sp'), lax.axis_index('cp')
+        sp = lax.axis_index('sp')
         rows = x_loc.shape[0] * cp_size
-        x_g = lax.all_gather(x_loc, 'cp', axis=0, tiled=True)
         cos_t, sin_t = rope_tables(cache_loc * seq_size + sp * rows + jnp.arange(rows))
+        qt, kv_rows, kv_head = front(x_loc, w_q, w_k, w_v, cos_t, sin_t, cp_size)
+        k_new = kv_rows[0].reshape(x_loc.shape[0], n_kv, HD)
+        v_new = kv_rows[1].reshape(x_loc.shape[0], n_kv, HD)
+        qt, kc_loc, vc_loc = lax.optimization_barrier((qt, kc_loc, vc_loc))
+        qt = lax.all_to_all(qt, 'sp', split_axis=0, concat_axis=1, tiled=True)
         kh = jnp.transpose(kc_loc, (1, 0, 2))
         vh = jnp.transpose(vc_loc, (1, 2, 0))
-        x_g, kh, vh = lax.optimization_barrier((x_g, kh, vh))
-        q_cols = w_q.shape[1] // cp_size
-        k_cols = w_k.shape[1] // cp_size
-        qoff = jnp.reshape(cp * (q_cols // BN_Q), (1,)).astype(jnp.int32)
-        koff = jnp.reshape(cp * (k_cols // 256), (1,)).astype(jnp.int32)
-        k_part = matmul(x_g, w_k, cos_t, sin_t, koff, k_cols, rope=True)
-        v_part = matmul(x_g, w_v, cos_t, sin_t, koff, k_cols, rope=False)
-        qt = matmul(x_g, w_q, cos_t, sin_t, qoff, q_cols, rope=True, trans=True, bn=BN_Q)
-        kv = jnp.stack([k_part, v_part], 0)
-        kv_rows = lax.all_to_all(kv, 'cp', split_axis=1, concat_axis=2, tiled=True)
-        k_new = kv_rows[0].reshape(x_loc.shape[0], n_kv, HD)
-        v_new = kv_rows[1].reshape(x_loc.shape[0], n_kv, HD)
-        kv_head = lax.all_to_all(kv, 'sp', split_axis=2, concat_axis=1, tiled=True)
-        qt = lax.all_to_all(qt, 'sp', split_axis=0, concat_axis=1, tiled=True)
         o_g = attention(kh, vh, qt, kv_head[0], kv_head[1].T)
         y_loc = out_project(o_g, w_o, cp_size, BN_O)
         return y_loc, k_new, v_new

time: 569 us -> 473 us (0.83)
  waiting for transfers between devices: 64.4 us -> 0.9 us
  between operations: 14.1 us -> 0.7 us
  starting transfers between devices: 11.5 us -> 3.77 us
  Pallas kernels: 444 us -> 437 us
    all_gather x1 -> x0, waiting for transfers between devices: 39.9 us -> none  [local_fn(): x_g = lax.all_gather(x_loc, 'cp', axis=0, tiled=True)]
    optimization_barrier x0 -> x2, local copies, waits for them, and re-layouts: none -> 19.6 us  [local_fn(): qt, kc_loc, vc_loc = lax.optimization_barrier((qt, kc_loc, vc_loc))]
    all_to_all x1, waiting for transfers between devices: 19.2 us -> 0.9 us  [local_fn(): qt = lax.all_to_all(qt, 'sp', split_axis=0, concat_axis=1, tiled=True)]
    unnamed x6, local copies, waits for them, and re-layouts: 23.3 us -> 5.39 us
    all_to_all x2 -> x0, starting transfers between devices: 7.48 us -> none  [the longest x1 4.04 us: local_fn(): kv_rows = lax.all_to_all(kv, 'cp', split_axis=1, concat_axis=2, tiled=True)]
    pallas_call x3 -> x1, Pallas kernels: 70.5 us -> 69.7 us  [front(): pl.pallas_call(functools.partial(front_kernel, kblk=kblk, chunk=chunk), i...]
  transfers between devices with their start and end apart: 4 -> 1, of which waited for: 3 -> 1; matrix products, arithmetic and copies ran while one was open for 5% -> 5% of each run, Pallas kernels for 10% -> 0%
where the time goes in v3:
time: 473 us; the launch traced here: 472 us
  Pallas kernels  437 us (92%)
  local copies, waits for them, and re-layouts  28.9 us (6%)
    pallas_call x1, Pallas kernels, attention(): pl.pallas_call(functools.partial(attn_kernel, tok=tok, group=group, kblk=...  314 us
    pallas_call x1, Pallas kernels, front(): pl.pallas_call(functools.partial(front_kernel, kblk=kblk, chunk=chunk), i...  69.7 us
    pallas_call x1, Pallas kernels, out_project(): pl.pallas_call(functools.partial(oproj_kernel, bn=bn, rows=rows // cp_siz...  52.5 us
    optimization_barrier x2, local copies, waits for them, and re-layouts, local_fn(): qt, kc_loc, vc_loc = lax.optimization_barrier((qt, kc_loc, vc_loc))  19.6 us
  transfers between devices with their start and end apart: 1, of which 1 were waited for; matrix products, arithmetic and copies ran while one was open for 5% of the time, Pallas kernels for 0%

profile of v3, /device:TPU:0, one launch (start us, length us, event | category | flops | bytes accessed | tf_op | source)
XLA Modules:
  0.0 472.3 jit_solution(12446884756158351664)
XLA Ops:
  0.7 0.5 fusion
  1.2 0.8 pad_maximum_fusion
  2.0 69.7 %shard_map.94 = (bf16[4096,256]{1,0:T(8,128)(2,1)}, bf16[2,64,1024]{2,1,0:T(8,128)(2,1)}, bf16[2,512,128]{2,1,0:T(8,128)(2,1)}) custom-call(bf16[64,16384]{1,0:T(8,128)(2,1)} %x_hbm.1, bf16[16384,16384]{1,0:T(8,128)(2,1)} %wq_hbm.1, bf16[16384,1024]{1,0:T(8,128)(2,1)} %wk_hbm.1, bf16[16384,1024]{1,0:T(8,128)(2,1)} %wv_hbm.1, ...), custom_call_target="tpu_custom_call" | custom-call | tf_op jit(solution)/shard_map/pallas_call | solution.py:167
  71.8 3.8 all-to-all-start
  75.6 1.1 copy.17
  76.7 1.0 slice_bitcast_fusion.1
  77.7 0.7 copy.20
  78.3 0.7 copy.19
  79.0 7.7 %copy.22 = bf16[4096,8,128]{2,0,1:T(8,128)(2,1)} copy(bf16[4096,8,128]{2,1,0:T(8,128)(2,1)} %param.8) | data formatting | bytes 16777216 | tf_op jit(solution)/shard_map/optimization_barrier | solution.py:471
  86.7 0.0 copy-start
  86.7 11.9 %copy.15 = bf16[4096,8,128]{0,2,1:T(8,128)(2,1)} copy(bf16[4096,8,128]{2,1,0:T(8,128)(2,1)} %param.9) | data formatting | bytes 16777216 | tf_op jit(solution)/shard_map/optimization_barrier | solution.py:471
  98.6 0.0 copy-done
  98.6 0.7 slice_bitcast_fusion.3.kn_ref
  99.3 0.7 slice_bitcast_fusion.vn_ref
  99.9 0.9 all-to-all-done
  100.8 1.5 copy.18
  102.3 314.4 %shard_map.95.x_hbm = bf16[256,16384]{1,0:T(8,128)(2,1)} custom-call(bf16[8,4096,128]{2,1,0:T(8,128)(2,1)} %bitcast.22, bf16[8,128,4096]{2,1,0:T(8,128)(2,1)} %bitcast.23, bf16[2048,512]{1,0:T(8,128)(2,1)} %bitcast.25, bf16[512,128]{1,0:T(8,128)(2,1)} %slice_bitcast_fusion.3.kn_ref, bf16[128,512]{1,0:T(8,128)(2,1)} %slice_bitcast_fusion.vn_ref), custom_call_target="tpu_custom_call" | custom-call | tf_op jit(solution)/shard_map/pallas_call | solution.py:354
  416.7 52.5 %shard_map.96 = bf16[64,16384]{1,0:T(8,128)(2,1)} custom-call(bf16[256,16384]{1,0:T(8,128)(2,1)} %shard_map.95.x_hbm, bf16[16384,16384]{1,0:T(8,128)(2,1)} %w_hbm.1), custom_call_target="tpu_custom_call" | custom-call | tf_op jit(solution)/shard_map/pallas_call | solution.py:440
  469.2 3.0 copy.24
  (2 shorter events, 0.0 us)
Async XLA Ops:
  71.8 29.0 %all-to-all-start = ((bf16[2,2048,256]{2,1,0:T(8,128)(2,1)}), bf16[2,2048,256]{2,1,0:T(8,128)(2,1)S(1)}, u32[]{:S(2)}, u32[]{:S(2)}) async-start(bf16[2,2048,256]{2,1,0:T(8,128)(2,1)} %bitcast.26), calls=%async_computation | async-start | bytes 4194304 | tf_op jit(solution)/shard_map/all_to_all | solution.py:472
  86.7 11.9 %copy-start = (bf16[2,512,128]{2,1,0:T(8,128)(2,1)S(1)}, bf16[2,512,128]{2,1,0:T(8,128)(2,1)}, u32[]{:S(2)}) copy-start(bf16[2,512,128]{2,1,0:T(8,128)(2,1)} %get-tuple-element.13) | copy-start | bytes 786436
